TPU v7x, 128 devices: a whole 4x4x4 slice. The times are simulated.
128 devices in a mesh: kv: 2 (over z_lo), batch: 64 (over z_hi, x, y, core).
Axes of the slice: x: 4, y: 4, z: 4 (z_hi: 2, z_lo: 2; z = z_hi * 2 + z_lo), core: 2. Of those that a mesh axis runs over, the one named last changes fastest.
Arguments:
- queries: bfloat16 [256, 32, 128], P(('kv', 'batch')), may hold values from -64 to 64
- prefix_keys: bfloat16 [8192, 8, 128], P('batch', 'kv'), may hold values from -6 to 6
- prefix_values: bfloat16 [8192, 8, 128], P('batch', 'kv'), may hold values from -6 to 6
- suffix_keys: bfloat16 [256, 2048, 8, 128], P('batch', None, 'kv'), may hold values from -6 to 6
- suffix_values: bfloat16 [256, 2048, 8, 128], P('batch', None, 'kv'), may hold values from -6 to 6
- suffix_lengths: int32 [256], P('batch'), may hold values from 512 to 2048, as said below
- slot_sequence: int32 [256], P('batch'), may hold values from 0 to 255, as said below
Outputs:
- attended: bfloat16 [256, 32, 128], P(('kv', 'batch'))
Inputs may be any that keep to these rules, and one draw needn't show every extreme that they name: `suffix_lengths`: some slot holds exactly 2048 live tokens. `slot_sequence`: each sequence's suffix occupies exactly one slot; the 256 / 64 slots of one index of batch hold sequences whose output rows lie on pairwise different indices of batch.
All inputs are finite; a program needn't handle non-finite values.
Results may differ from a plain program's by a relative error of at most 0.007.
Values may be sent and summed in bfloat16 or wider, within the bound.
No kernel may reach another device: no remote copies, remote signals or barrier semaphores. Data moves between devices by JAX's collectives and lax.ppermute only.
A program may use at most 64 MiB of HBM per device.

v0:
```python
import jax
import jax.numpy as jnp
from jax import lax
from jax.sharding import PartitionSpec as P

negative_fill = -1e30


def sent_to_all(value, axis):
    copies = jnp.broadcast_to(value, (lax.axis_size(axis), *value.shape))
    return lax.all_to_all(copies, axis, split_axis=0, concat_axis=0, tiled=True)


def joined_along(pieces, dim):
    lengths = list(pieces.shape[1:])
    lengths[dim] *= pieces.shape[0]
    return jnp.moveaxis(pieces, 0, dim).reshape(lengths)


def collect(value, axis, dim):
    pieces = sent_to_all(value, axis)
    return joined_along(pieces, dim)


def cut_along(value, dim, count):
    before, after = (value.shape[:dim], value.shape[dim + 1 :])
    return jnp.moveaxis(value.reshape(*before, count, -1, *after), dim, 0)


def exchange_both(value, axis, axes, splits, concats):
    sizes = [lax.axis_size(a) for a in axes]
    pieces = cut_along(value, splits[0], sizes[0])
    pieces = jnp.moveaxis(cut_along(pieces, splits[1] + 1, sizes[1]), 0, 1)
    inside = pieces.shape[2:]
    pieces = pieces.reshape(-1, *inside)
    pieces = lax.all_to_all(pieces, axis, split_axis=0, concat_axis=0, tiled=True)
    pieces = joined_along(pieces.reshape(*sizes, *inside), concats[0] + 1)
    return joined_along(pieces, concats[1])


def fold_block(state, keys_part, values_part, grouped, scale):
    best, total, accum = state
    scores = (
        jnp.einsum("rkjd,tkd->rkjt", grouped, keys_part, preferred_element_type=jnp.float32) * scale
    )
    new_best = jnp.maximum(best, jnp.max(scores, axis=-1))
    weights = jnp.exp(scores - new_best[..., None])
    total = jnp.sum(weights, axis=-1)
    accum = jnp.einsum(
        "rkjt,tkd->rkjd",
        weights.astype(jnp.bfloat16),
        values_part,
        preferred_element_type=jnp.float32,
    )
    return (new_best, total, accum)


def merge_rows(best, total, accum, row_ids, part_best, part_total, part_acc):
    old_best = best[row_ids]
    new_best = jnp.maximum(old_best, part_best)
    first = jnp.exp(old_best - new_best)
    second = jnp.exp(part_best - new_best)
    best = best.at[row_ids].set(new_best)
    total = total.at[row_ids].set(total[row_ids] * first + part_total * second)
    accum = accum.at[row_ids].set(accum[row_ids] * first[..., None] + part_acc * second[..., None])
    return (best, total, accum)


def shards(
    queries, prefix_keys, prefix_values, suffix_keys, suffix_values, suffix_lengths, slot_sequence
):
    kv_count = lax.axis_size("kv")
    batch_count = lax.axis_size("batch")
    per_device = queries.shape[0]
    head_count = queries.shape[1]
    head_dim = queries.shape[2]
    local_heads = head_count // kv_count
    kv_local = prefix_keys.shape[1]
    group_size = local_heads // kv_local
    scale = head_dim ** (-0.5)
    relayed = lax.all_to_all(queries, "kv", split_axis=1, concat_axis=0, tiled=True)
    gathered = collect(relayed, "batch", 0)
    batch_total = gathered.shape[0]
    everyone = gathered.reshape(batch_count, kv_count, per_device, local_heads, head_dim)
    everyone = everyone.transpose(1, 0, 2, 3, 4).reshape(batch_total, local_heads, head_dim)
    slots = suffix_keys.shape[0]
    suffix_len = suffix_keys.shape[1]
    slot_queries = jnp.take(everyone, slot_sequence, axis=0).reshape(
        slots, kv_local, group_size, head_dim
    )
    scores = (
        jnp.einsum("skjd,stkd->skjt", slot_queries, suffix_keys, preferred_element_type=jnp.float32)
        * scale
    )
    position = jnp.arange(suffix_len)
    scores = jnp.where(
        position[None, None, None, :] < suffix_lengths[:, None, None, None], scores, negative_fill
    )
    suf_best = jnp.max(scores, axis=-1)
    weights = jnp.exp(scores - suf_best[..., None])
    suf_total = jnp.sum(weights, axis=-1)
    suf_acc = jnp.einsum(
        "skjt,stkd->skjd",
        weights.astype(jnp.bfloat16),
        suffix_values,
        preferred_element_type=jnp.float32,
    )
    grouped_all = everyone.reshape(batch_total, kv_local, group_size, head_dim)
    start_state = (
        jnp.full((batch_total, kv_local, group_size), negative_fill, jnp.float32),
        jnp.zeros((batch_total, kv_local, group_size), jnp.float32),
        jnp.zeros((batch_total, kv_local, group_size, head_dim), jnp.float32),
    )
    best, total, accum = fold_block(start_state, prefix_keys, prefix_values, grouped_all, scale)
    best, total, accum = merge_rows(best, total, accum, slot_sequence, suf_best, suf_total, suf_acc)
    got_acc, got_best, got_total = (
        exchange_both(
            accum.reshape(batch_total, 1, local_heads, head_dim),
            ("kv", "batch"),
            ("kv", "batch"),
            (0, 0),
            (2, 1),
        ),
        exchange_both(
            best.reshape(batch_total, 1, local_heads),
            ("kv", "batch"),
            ("kv", "batch"),
            (0, 0),
            (2, 1),
        ),
        exchange_both(
            total.reshape(batch_total, 1, local_heads),
            ("kv", "batch"),
            ("kv", "batch"),
            (0, 0),
            (2, 1),
        ),
    )
    top = jnp.max(got_best, axis=1)
    factor = jnp.exp(got_best - top[:, None, :])
    denominator = jnp.sum(got_total * factor, axis=1)
    numerator = jnp.sum(got_acc * factor[..., None], axis=1)
    return (numerator / denominator[..., None]).astype(jnp.bfloat16)


def solution(mesh):
    return jax.shard_map(
        shards,
        mesh=mesh,
        in_specs=(
            P(("kv", "batch"), None, None),
            P("batch", "kv", None),
            P("batch", "kv", None),
            P("batch", None, "kv", None),
            P("batch", None, "kv", None),
            P("batch"),
            P("batch"),
        ),
        out_specs=P(("kv", "batch"), None, None),
        check_vma=False,
    )
```

profile of v0, /device:TPU:1, one launch (start us, length us, event | category | flops | bytes accessed | tf_op | source)
XLA Modules:
  0.0 123.4 jit_solution(10808240122863264422)
XLA Ops:
  0.0 0.8 copy.99
  0.8 6.2 %all_to_all.38 = bf16[2,32,128]{2,0,1:T(2,128)(2,1)S(1)} all-to-all(bf16[2,32,128]{2,0,1:T(2,128)(2,1)S(1)} %copy.99), channel_id=1, replica_groups=mesh['kv'=2,'batch'=64] {'kv'}, dimensions={1} | all-to-all | bytes 32768 | tf_op jit(solution)/shard_map/all_to_all | solution.py:81
  7.0 1.2 %broadcast_in_dim.28 = bf16[64,4,16,128]{3,2,1,0:T(8,128)(2,1)} broadcast(bf16[4,16,128]{2,1,0:T(8,128)(2,1)S(1)} %bitcast.82), dimensions={1,2,3} | broadcast | bytes 1064960 | tf_op jit(solution)/shard_map/broadcast_in_dim | solution.py:10
  8.3 12.6 %all-to-all-start.1 = ((bf16[64,4,16,128]{3,2,1,0:T(8,128)(2,1)}), bf16[64,4,16,128]{3,2,1,0:T(8,128)(2,1)S(1)}, u32[]{:S(2)}, u32[]{:S(2)}) async-start(bf16[64,4,16,128]{3,2,1,0:T(8,128)(2,1)} %broadcast_in_dim.28), calls=%async_computation.1 | async-start | bytes 2097152 | tf_op jit(solution)/shard_map/all_to_all | solution.py:11
  21.0 18.5 %all-to-all-done.1 = bf16[64,4,16,128]{3,2,1,0:T(8,128)(2,1)S(1)} async-done(((bf16[64,4,16,128]{3,2,1,0:T(8,128)(2,1)}), bf16[64,4,16,128]{3,2,1,0:T(8,128)(2,1)S(1)}, u32[]{:S(2)}, u32[]{:S(2)}) %all-to-all-start.1) | async-done | bytes 1048608 | tf_op jit(solution)/shard_map/all_to_all | solution.py:11
  39.5 1.1 copy.108
  40.6 1.1 copy.102
  41.7 0.5 bitcast_reduce_fusion
  42.5 0.4 fusion.11
  42.9 1.8 %gather_fusion.2 = bf16[4,16,128]{2,1,0:T(8,128)(2,1)S(1)} fusion(bf16[256,16,128]{2,1,0:T(8,128)(2,1)} %bitcast.74, s32[1024]{0:T(1024)S(1)} %pad_clamp_fusion), kind=kCustom, calls=%fused_computation.2 | custom fusion | bytes 32784 | tf_op jit(solution)/shard_map/jit(_take)/gather | solution.py:88
  44.7 0.6 gather_fusion.1
  45.5 0.6 gather_fusion.3
  46.1 5.8 %fusion.35 = (f32[4,4,4]{2,1,0:T(4,128)S(1)}, f32[4,4,4,2048]{3,2,1,0:T(4,128)S(1)}) fusion(bf16[4,2048,4,128]{3,2,1,0:T(4,128)(2,1)} %param.10, bf16[4,4,4,128]{3,2,1,0:T(4,128)(2,1)S(1)} %bitcast.90, pred[4]{0:T(512)(128)(4,1)S(1)} %compare_and_fusion, pred[4,2048]{1,0:T(4,128)(4,1)S(1)} %iota_compare_fusion), kind=kOutput, calls=%fused_computation.48 | convolution fusion | flops 33955776 | bytes 8937732 | tf_op jit(solution)/shard_map/skjd,stkd->skjt/dot_general | solution.py:92
  51.8 0.3 fusion.22
  52.2 0.5 copy-done.1
  52.6 0.6 scatter_fusion.1
  53.3 1.0 reshape_reshape_reshape_reshape.10
  54.3 4.1 %all-to-all-start.3 = ((f32[128,2,1,16]{3,1,2,0:T(2,128)}), f32[128,2,1,16]{3,1,2,0:T(2,128)S(1)}, u32[]{:S(2)}, u32[]{:S(2)}) async-start(f32[128,2,1,16]{3,1,2,0:T(2,128)} %bitcast.20), calls=%async_computation.3 | async-start | bytes 262144 | tf_op jit(solution)/shard_map/all_to_all | solution.py:36
  58.4 0.6 convolution_bitcast_fusion
  59.0 2.7 %copy.111 = f32[256,4,4,128]{3,2,1,0:T(4,128)} copy(f32[256,4,4,128]{3,0,2,1:T(8,128)S(1)} %convolution_bitcast_fusion) | data formatting | bytes 4194304 | tf_op jit(solution)/shard_map/rkjt,tkd->rkjd/transpose | solution.py:49
  61.7 2.2 %gather_fusion = f32[4,4,4,128]{3,2,1,0:T(4,128)S(1)} fusion(f32[256,4,4,128]{3,2,1,0:T(4,128)} %copy.111, s32[1024]{0:T(1024)S(1)} %pad_clamp_fusion), kind=kCustom, calls=%fused_computation | custom fusion | bytes 65552 | tf_op jit(solution)/shard_map/gather | solution.py:65
  63.9 0.6 scatter_fusion.2
  64.5 1.0 reshape_reshape_reshape_reshape.11
  65.5 2.9 %all-to-all-done.3 = f32[128,2,1,16]{3,1,2,0:T(2,128)S(1)} async-done(((f32[128,2,1,16]{3,1,2,0:T(2,128)}), f32[128,2,1,16]{3,1,2,0:T(2,128)S(1)}, u32[]{:S(2)}, u32[]{:S(2)}) %all-to-all-start.3) | async-done | bytes 16416 | tf_op jit(solution)/shard_map/all_to_all | solution.py:36
  68.4 6.8 %all-to-all-start.4 = ((f32[128,2,1,16]{3,1,2,0:T(2,128)}), f32[128,2,1,16]{3,1,2,0:T(2,128)S(1)}, u32[]{:S(2)}, u32[]{:S(2)}) async-start(f32[128,2,1,16]{3,1,2,0:T(2,128)} %bitcast.27), calls=%async_computation.4 | async-start | bytes 262144 | tf_op jit(solution)/shard_map/all_to_all | solution.py:36
  75.3 4.7 %fusion.16 = f32[4,4,4,128]{3,2,1,0:T(4,128)S(1)} fusion(bf16[4,2048,4,128]{3,2,1,0:T(4,128)(2,1)} %param.11, f32[4,4,4,2048]{3,2,1,0:T(4,128)S(1)} %copy-done.2, f32[4,4,4]{2,1,0:T(4,128)S(1)} %get-tuple-element.11, f32[4,4,4,128]{3,2,1,0:T(4,128)S(1)} %gather_fusion, f32[4,4,4]{2,1,0:T(4,128)S(1)} %bitcast.92, f32[4,4,4]{2,1,0:T(4,128)S(1)} %bitcast.91), kind=kOutput, calls=%fused_computation.21 | convolution fusion | flops 33841152 | bytes 8979200 | tf_op jit(solution)/shard_map/skjt,stkd->skjd/dot_general | solution.py:102
  79.9 1.9 %scatter_fusion = f32[256,4,4,128]{3,2,1,0:T(4,128)} fusion(f32[256,4,4,128]{3,2,1,0:T(4,128)} %copy.111, s32[4]{0:T(128)S(1)} %compare_select_fusion, f32[4,4,4,128]{3,2,1,0:T(4,128)S(1)} %fusion.16), kind=kCustom, calls=%fused_computation.4 | custom fusion | bytes 98320 | tf_op jit(solution)/shard_map/scatter | solution.py:65
  81.9 3.5 %all-to-all-done.4 = f32[128,2,1,16]{3,1,2,0:T(2,128)S(1)} async-done(((f32[128,2,1,16]{3,1,2,0:T(2,128)}), f32[128,2,1,16]{3,1,2,0:T(2,128)S(1)}, u32[]{:S(2)}, u32[]{:S(2)}) %all-to-all-start.4) | async-done | bytes 16416 | tf_op jit(solution)/shard_map/all_to_all | solution.py:36
  85.3 6.3 %all-to-all-start.2 = ((f32[128,2,1,16,128]{4,3,1,2,0:T(8,128)}), f32[128,2,1,16,128]{4,3,1,2,0:T(8,128)S(1)}, u32[]{:S(2)}, u32[]{:S(2)}) async-start(f32[128,2,1,16,128]{4,3,1,2,0:T(8,128)} %bitcast.14), calls=%async_computation.2 | async-start | bytes 4194304 | tf_op jit(solution)/shard_map/all_to_all | solution.py:36
  92.2 29.5 %all-to-all-done.2 = f32[128,2,1,16,128]{4,3,1,2,0:T(8,128)S(1)} async-done(((f32[128,2,1,16,128]{4,3,1,2,0:T(8,128)}), f32[128,2,1,16,128]{4,3,1,2,0:T(8,128)S(1)}, u32[]{:S(2)}, u32[]{:S(2)}) %all-to-all-start.2) | async-done | bytes 2097184 | tf_op jit(solution)/shard_map/all_to_all | solution.py:36
  122.0 0.7 multiply_reduce_fusion
  122.7 0.7 divide_convert_fusion
  (30 shorter events, 1.5 us)
Async XLA Ops:
  0.0 58.4 %copy-start = (bf16[128,4,128]{2,1,0:T(4,128)(2,1)S(1)}, bf16[128,4,128]{2,1,0:T(4,128)(2,1)}, u32[]{:S(2)}) copy-start(bf16[128,4,128]{2,1,0:T(4,128)(2,1)} %param.9) | copy-start | bytes 393220
  0.0 20.9 %copy-start.5 = (s32[4]{0:T(128)S(1)}, s32[4]{0:T(128)}, u32[]{:S(2)}) copy-start(s32[4]{0:T(128)} %param.13) | copy-start | bytes 52
  0.0 20.9 %copy-start.4 = (s32[4]{0:T(128)S(1)}, s32[4]{0:T(128)}, u32[]{:S(2)}) copy-start(s32[4]{0:T(128)} %param.12) | copy-start | bytes 52
  8.3 31.2 %all-to-all-start.1 = ((bf16[64,4,16,128]{3,2,1,0:T(8,128)(2,1)}), bf16[64,4,16,128]{3,2,1,0:T(8,128)(2,1)S(1)}, u32[]{:S(2)}, u32[]{:S(2)}) async-start(bf16[64,4,16,128]{3,2,1,0:T(8,128)(2,1)} %broadcast_in_dim.28), calls=%async_computation.1 | async-start | bytes 2097152 | tf_op jit(solution)/shard_map/all_to_all | solution.py:11
  39.5 2.2 %copy-start.3 = (bf16[128,4,128]{2,1,0:T(4,128)(2,1)S(1)}, bf16[128,4,128]{2,1,0:T(4,128)(2,1)}, u32[]{:S(2)}) copy-start(bf16[128,4,128]{2,1,0:T(4,128)(2,1)} %param.8) | copy-start | bytes 393220
  51.8 0.8 copy-start.1
  54.3 14.2 %all-to-all-start.3 = ((f32[128,2,1,16]{3,1,2,0:T(2,128)}), f32[128,2,1,16]{3,1,2,0:T(2,128)S(1)}, u32[]{:S(2)}, u32[]{:S(2)}) async-start(f32[128,2,1,16]{3,1,2,0:T(2,128)} %bitcast.20), calls=%async_computation.3 | async-start | bytes 262144 | tf_op jit(solution)/shard_map/all_to_all | solution.py:36
  59.0 16.3 %copy-start.2 = (f32[4,4,4,2048]{3,2,1,0:T(4,128)S(1)}, f32[4,4,4,2048]{3,2,1,0:T(4,128)}, u32[]{:S(2)}) copy-start(f32[4,4,4,2048]{3,2,1,0:T(4,128)} %copy-done.1) | copy-start | bytes 1572868
  68.4 16.9 %all-to-all-start.4 = ((f32[128,2,1,16]{3,1,2,0:T(2,128)}), f32[128,2,1,16]{3,1,2,0:T(2,128)S(1)}, u32[]{:S(2)}, u32[]{:S(2)}) async-start(f32[128,2,1,16]{3,1,2,0:T(2,128)} %bitcast.27), calls=%async_computation.4 | async-start | bytes 262144 | tf_op jit(solution)/shard_map/all_to_all | solution.py:36
  85.3 36.4 %all-to-all-start.2 = ((f32[128,2,1,16,128]{4,3,1,2,0:T(8,128)}), f32[128,2,1,16,128]{4,3,1,2,0:T(8,128)S(1)}, u32[]{:S(2)}, u32[]{:S(2)}) async-start(f32[128,2,1,16,128]{4,3,1,2,0:T(8,128)} %bitcast.14), calls=%async_computation.2 | async-start | bytes 4194304 | tf_op jit(solution)/shard_map/all_to_all | solution.py:36
where the time goes:
time: 124 us; the launch traced here: 123 us
  waiting for transfers between devices  54.4 us (44%)
  starting transfers between devices  29.8 us (24%)
  local copies, waits for them, and re-layouts  18.7 us (15%)
  matrix products  11.5 us (9%)
  blocking collectives  6.23 us (5%)
  other arithmetic  2.52 us (2%)
    all_to_all x3, waiting for transfers between devices, exchange_both(): lax.all_to_all(pieces, axis, split_axis=0, concat_axis=0, tiled=True)  35.9 us
    all_to_all x1, waiting for transfers between devices, sent_to_all(): return lax.all_to_all(copies, axis, split_axis=0, concat_axis=0, tiled=True)  18.5 us
    all_to_all x3, starting transfers between devices, exchange_both(): lax.all_to_all(pieces, axis, split_axis=0, concat_axis=0, tiled=True)  17.2 us
    all_to_all x1, starting transfers between devices, sent_to_all(): return lax.all_to_all(copies, axis, split_axis=0, concat_axis=0, tiled=True)  12.6 us
    all_to_all x1, blocking collectives, shards(): lax.all_to_all(queries, 'kv', split_axis=1, concat_axis=0, tiled=True)  6.23 us
    dot_general x1, matrix products, shards(): jnp.einsum('skjd,stkd->skjt', slot_queries, suffix_keys, preferred_elemen...  5.78 us
    dot_general x1, matrix products, shards(): jnp.einsum('skjt,stkd->skjd', weights.astype(jnp.bfloat16), suffix_values...  4.66 us
    transpose x1, local copies, waits for them, and re-layouts, fold_block(): jnp.einsum('rkjt,tkd->rkjd', weights.astype(jnp.bfloat16), values_part, p...  2.7 us
  transfers between devices with their start and end apart: 4, of which 4 were waited for; matrix products, arithmetic and copies ran while one was open for 12% of the time, Pallas kernels for 0%

commit v1 on v0

v1 whole, which is shorter than its diff:
```python
import jax
import jax.numpy as jnp
from jax import lax
from jax.experimental import pallas as pl
from jax.experimental.pallas import tpu as pltpu
from jax.sharding import Mesh
from jax.sharding import PartitionSpec as P

negative_fill = -1e30
f32 = jnp.float32
bf16 = jnp.bfloat16
vmem = pl.BlockSpec(memory_space=pltpu.VMEM)
smem = pl.BlockSpec(memory_space=pltpu.SMEM)


def limit(mib):
    return pltpu.CompilerParams(vmem_limit_bytes=mib << 20)


def rounded(x):
    return x.astype(bf16).astype(f32)


def nt_dot(a, b):
    return lax.dot_general(a, b, (((1,), (1,)), ((), ())), preferred_element_type=f32)


def ask_kernel(queries_ref, out_ref):
    groups, copies = out_ref.shape[:2]
    sub8 = lax.broadcasted_iota(jnp.int32, (8, out_ref.shape[3]), 0)
    for g in range(groups):
        tiles = []
        for k in (0, 2):
            base = 16 * g + 4 * k
            one = queries_ref[0, base : base + 8, :].astype(f32)
            two = queries_ref[1, base : base + 8, :].astype(f32)
            tiles.append(jnp.where(sub8 < 4, one, pltpu.roll(two, 4, 0)))
            tiles.append(jnp.where(sub8 < 4, pltpu.roll(one, 4, 0), two))
        piece = jnp.concatenate(tiles, axis=0).astype(bf16)
        for c in range(copies):
            out_ref[g, c] = piece


def prefix_kernel(q_ref, k0_ref, k1_ref, v0_ref, v1_ref, out_ref):
    pieces = q_ref.shape[0]
    kv_local, _, dim = k0_ref.shape
    scale = dim ** (-0.5)
    rows = pieces * 8
    lane = lax.broadcasted_iota(jnp.int32, (rows, 128), 1)
    stat = jnp.zeros((rows, 128), f32)
    for k in range(kv_local):
        q = q_ref[:, 8 * k : 8 * k + 8, :].astype(f32).reshape(rows, dim).astype(bf16)
        keys = jnp.concatenate([k0_ref[k], k1_ref[k]], axis=0)
        values = jnp.concatenate([v0_ref[k], v1_ref[k]], axis=0)
        scores = nt_dot(q, keys) * scale
        best = rounded(jnp.max(scores, axis=1, keepdims=True))
        weights = jnp.exp(scores - best)
        total = jnp.sum(weights, axis=1, keepdims=True)
        acc = jnp.dot(weights.astype(bf16), values, preferred_element_type=f32)
        out_ref[:, 8 * k : 8 * k + 8, :] = acc.reshape(pieces, 8, dim).astype(bf16)
        high = rounded(total)
        stat = jnp.where(lane == 4 * k, best, stat)
        stat = jnp.where(lane == 4 * k + 1, high, stat)
        stat = jnp.where(lane == 4 * k + 2, total - high, stat)
    out_ref[:, 8 * kv_local : 8 * kv_local + 8, :] = stat.reshape(pieces, 8, 128).astype(bf16)


def place_of(sequence, batch_count, per_device):
    device = sequence // per_device
    return device // 2, device % 2, sequence % per_device


def suffix_kernel(ids_ref, len_ref, mine_ref, other_ref, keys_ref, values_ref, out_ref):
    slots, wide, dim = keys_ref.shape
    scale = dim ** (-0.5)
    chunk = 1024
    row = lax.broadcasted_iota(jnp.int32, (16, chunk), 0)
    lane = lax.broadcasted_iota(jnp.int32, (16, chunk), 1)
    own_head = lane % 4 == row // 4
    position = lane // 4
    sub8 = lax.broadcasted_iota(jnp.int32, (8, dim), 0)
    lane8 = lax.broadcasted_iota(jnp.int32, (8, dim), 1)
    for s in range(slots):
        piece, core, i = place_of(ids_ref[s], 0, 2)
        length = len_ref[s]
        here = core == lax.axis_index("core")
        q = jnp.where(here, mine_ref[piece].astype(f32), other_ref[piece].astype(f32))
        pairs = []
        for k in (0, 2):
            even, odd = q[8 * k : 8 * k + 8], q[8 * k + 8 : 8 * k + 16]
            even = jnp.where(i == 0, even, pltpu.roll(even, 4, 0))
            odd = jnp.where(i == 0, pltpu.roll(odd, 4, 0), odd)
            pairs.append(jnp.where(sub8 < 4, even, odd))
        q16 = jnp.concatenate(pairs, axis=0).astype(bf16)
        parts = []
        peak = jnp.full((16, 128), negative_fill, f32)
        for c in range(wide // chunk):
            part = nt_dot(q16, keys_ref[s, c * chunk : (c + 1) * chunk, :]) * scale
            keep = own_head & (position < length - c * (chunk // 4))
            part = jnp.where(keep, part, negative_fill)
            for t in range(chunk // 128):
                peak = jnp.maximum(peak, part[:, 128 * t : 128 * t + 128])
            parts.append(part)
        best = rounded(jnp.max(peak, axis=1, keepdims=True))
        sums = jnp.zeros((16, 128), f32)
        acc = jnp.zeros((16, dim), f32)
        for c in range(wide // chunk):
            weights = jnp.exp(parts[c] - best)
            for t in range(chunk // 128):
                sums = sums + weights[:, 128 * t : 128 * t + 128]
            acc = acc + jnp.dot(
                weights.astype(bf16),
                values_ref[s, c * chunk : (c + 1) * chunk, :],
                preferred_element_type=f32,
            )
        total = jnp.sum(sums, axis=1, keepdims=True)
        best, total = jnp.broadcast_to(best, (16, dim)), jnp.broadcast_to(total, (16, dim))
        stat = jnp.zeros((8, dim), f32)
        for k in range(4):
            half = slice(8 * (k // 2), 8 * (k // 2) + 8)

            def spread(x):
                x = x[half]
                return jnp.where(i == k % 2, x, pltpu.roll(x, 4, 0))

            out_ref[s, 8 * k : 8 * k + 8, :] = spread(acc)
            stat = jnp.where(lane8 == 4 * k, spread(best), stat)
            stat = jnp.where(lane8 == 4 * k + 1, spread(total), stat)
        out_ref[s, 32:40, :] = stat


def merge_kernel(ids_ref, ids_other_ref, part_ref, mine_ref, other_ref, out_ref):
    del part_ref
    sub8 = lax.broadcasted_iota(jnp.int32, (8, 128), 0)
    lane8 = lax.broadcasted_iota(jnp.int32, (8, 128), 1)

    def one(ids, results, s):
        piece, core, i = place_of(ids[s], 0, 2)

        @pl.when(core == lax.axis_index("core"))
        def _():
            used = sub8 // 4 == i
            old = out_ref[piece, 32:40, :].astype(f32)
            new = results[s, 32:40, :]
            stat = old
            for k in range(4):
                best_old, high, low = (old[:, 4 * k + c : 4 * k + c + 1] for c in range(3))
                best_new, total_new = (new[:, 4 * k + c : 4 * k + c + 1] for c in range(2))
                best = jnp.maximum(best_old, best_new)
                first = jnp.broadcast_to(jnp.exp(best_old - best), (8, 128))
                second = jnp.broadcast_to(jnp.exp(best_new - best), (8, 128))
                total = (high + low) * first + total_new * second
                acc_old = out_ref[piece, 8 * k : 8 * k + 8, :].astype(f32)
                acc = acc_old * first + results[s, 8 * k : 8 * k + 8, :] * second
                out_ref[piece, 8 * k : 8 * k + 8, :] = jnp.where(used, acc, acc_old).astype(bf16)
                rest = rounded(total)
                stat = jnp.where(used & (lane8 == 4 * k), best, stat)
                stat = jnp.where(used & (lane8 == 4 * k + 1), rest, stat)
                stat = jnp.where(used & (lane8 == 4 * k + 2), total - rest, stat)
            out_ref[piece, 32:40, :] = stat.astype(bf16)

    for s in range(mine_ref.shape[0]):
        one(ids_ref, mine_ref, s)
        one(ids_other_ref, other_ref, s)


def combine_kernel(got_ref, out_ref):
    count = got_ref.shape[0] // 2
    sub8 = lax.broadcasted_iota(jnp.int32, (8, 128), 0)
    for half in range(2):
        at = slice(half * count, (half + 1) * count)
        stat = got_ref[at, 32:40, :].astype(f32)
        top = jnp.max(stat, axis=0, keepdims=True)
        factor = jnp.exp(stat - top)
        total = pltpu.roll(stat, 127, 2) + pltpu.roll(stat, 126, 2)
        factor = factor / jnp.sum(factor * total, axis=0, keepdims=True)
        rows = []
        for k in range(4):
            acc = got_ref[at, 8 * k : 8 * k + 8, :].astype(f32)
            rows.append(jnp.sum(acc * factor[:, :, 4 * k : 4 * k + 1], axis=0))
        for k in (0, 2):
            base = 16 * half + 4 * k
            turned = pltpu.roll(rows[k + 1], 4, 0)
            out_ref[0, base : base + 8, :] = jnp.where(sub8 < 4, rows[k], turned).astype(bf16)
            turned = pltpu.roll(rows[k], 4, 0)
            out_ref[1, base : base + 8, :] = jnp.where(sub8 < 4, turned, rows[k + 1]).astype(bf16)


def shards(
    queries, prefix_keys, prefix_values, suffix_keys, suffix_values, suffix_lengths, slot_sequence
):
    kv_count = lax.axis_size("kv")
    m_count = lax.axis_size("m")
    per_device, head_count, dim = queries.shape
    local_heads = head_count // kv_count
    kv_local = prefix_keys.shape[1]
    group = local_heads // kv_local
    pieces = kv_count * m_count
    slots, suffix_len = suffix_keys.shape[:2]
    swap = [(0, 1), (1, 0)]

    def across(x):
        return lax.ppermute(x, "core", swap)

    def exchange(x):
        return lax.all_to_all(x, ("kv", "m"), split_axis=0, concat_axis=0, tiled=True)

    sent = pl.pallas_call(
        ask_kernel,
        in_specs=[vmem],
        out_specs=vmem,
        out_shape=jax.ShapeDtypeStruct((kv_count, m_count, per_device * local_heads, dim), bf16),
        cost_estimate=pl.CostEstimate(flops=10**11, transcendentals=0, bytes_accessed=2**28),
        compiler_params=limit(4),
        name="ask",
    )(queries)
    mine = exchange(sent.reshape(pieces, per_device * local_heads, dim))

    keys = suffix_keys.reshape(slots, suffix_len * kv_local, dim)
    values = suffix_values.reshape(slots, suffix_len * kv_local, dim)
    keys_here, values_here = prefix_keys.transpose(1, 0, 2), prefix_values.transpose(1, 0, 2)
    keys_there, values_there = across(keys_here), across(values_here)
    ids_there = across(slot_sequence)

    other = across(mine)
    part = pl.pallas_call(
        prefix_kernel,
        in_specs=[vmem] * 5,
        out_specs=vmem,
        out_shape=jax.ShapeDtypeStruct((pieces, per_device * local_heads + 8, dim), bf16),
        cost_estimate=pl.CostEstimate(flops=10**9, transcendentals=0, bytes_accessed=2**21),
        compiler_params=limit(4),
        name="prefix",
    )(mine, keys_here, keys_there, values_here, values_there)

    found = pl.pallas_call(
        suffix_kernel,
        in_specs=[smem] * 2 + [vmem] * 4,
        out_specs=vmem,
        out_shape=jax.ShapeDtypeStruct((slots, per_device * local_heads + 8, dim), f32),
        cost_estimate=pl.CostEstimate(flops=10**9, transcendentals=0, bytes_accessed=2**21),
        compiler_params=limit(4),
        name="suffix",
    )(slot_sequence, suffix_lengths, mine, other, keys, values)
    found_there = across(found)

    part = pl.pallas_call(
        merge_kernel,
        in_specs=[smem] * 2 + [vmem] * 3,
        out_specs=vmem,
        out_shape=jax.ShapeDtypeStruct(part.shape, bf16),
        input_output_aliases={2: 0},
        compiler_params=limit(4),
        name="merge",
    )(slot_sequence, ids_there, part, found, found_there)

    got = exchange(part)
    return pl.pallas_call(
        combine_kernel,
        in_specs=[vmem],
        out_specs=vmem,
        out_shape=jax.ShapeDtypeStruct(queries.shape, bf16),
        compiler_params=limit(4),
        name="combine",
    )(got)


def solution(mesh):
    kv, batch = (mesh.shape[a] for a in ("kv", "batch"))
    fine = Mesh(mesh.devices.reshape(kv, batch // 2, 2), ("kv", "m", "core"))
    rows, positions = ("kv", "m", "core"), ("m", "core")
    return jax.shard_map(
        shards,
        mesh=fine,
        in_specs=(
            P(rows, None, None),
            P(positions, "kv", None),
            P(positions, "kv", None),
            P(positions, None, "kv", None),
            P(positions, None, "kv", None),
            P(positions),
            P(positions),
        ),
        out_specs=P(rows, None, None),
        check_vma=False,
    )
```

time: 124 us -> 56.5 us (0.46)
  waiting for transfers between devices: 54.4 us -> 0.72 us
  blocking collectives: 6.23 us -> 42.3 us
  starting transfers between devices: 29.8 us -> 3.19 us
  local copies, waits for them, and re-layouts: 18.7 us -> 0.92 us
  matrix products: 11.5 us -> 0 us
  Pallas kernels: 0 us -> 8.53 us
  other arithmetic: 2.52 us -> 0 us
    all_to_all x4 -> x0, waiting for transfers between devices: 54.4 us -> none  [the longest x3 35.9 us: exchange_both(): lax.all_to_all(pieces, axis, split_axis=0, concat_axis=0, tiled=True)]
    all_to_all x1 -> x2, blocking collectives: 6.23 us -> 42.3 us  [exchange(): lax.all_to_all(x, ('kv', 'm'), split_axis=0, concat_axis=0, tiled=True)]
    all_to_all x4 -> x0, starting transfers between devices: 29.8 us -> none  [the longest x3 17.2 us: exchange_both(): lax.all_to_all(pieces, axis, split_axis=0, concat_axis=0, tiled=True)]
    dot_general x4 -> x0, matrix products: 11.5 us -> none  [the longest x1 5.78 us: shards(): jnp.einsum('skjd,stkd->skjt', slot_queries, suffix_keys, preferred_elemen...]
    pallas_call x0 -> x5, Pallas kernels: none -> 8.53 us  [the longest x1 4.84 us: shards(): pl.pallas_call(suffix_kernel, in_specs=[smem] * 2 + [vmem] * 4, out_specs...]
    transpose x6 -> x0, local copies, waits for them, and re-layouts: 5.18 us -> none  [the longest x1 2.7 us: fold_block(): jnp.einsum('rkjt,tkd->rkjd', weights.astype(jnp.bfloat16), values_part, p...]
    gather x4 -> x0, local copies, waits for them, and re-layouts: 5.09 us -> none  [the longest x1 2.17 us: merge_rows(): accum[row_ids] * first[..., None] + part_acc * second[..., None]]
    ppermute x0 -> x5, starting transfers between devices: none -> 3.19 us  [across(): return lax.ppermute(x, 'core', swap)]
  transfers between devices with their start and end apart: 4 -> 5, of which waited for: 4 -> 1; matrix products, arithmetic and copies ran while one was open for 12% -> 0% of each run, Pallas kernels for 0% -> 11%
where the time goes in v1:
time: 56.5 us; the launch traced here: 55.8 us
  blocking collectives  42.3 us (75%)
  Pallas kernels  8.53 us (15%)
  starting transfers between devices  3.19 us (6%)
  local copies, waits for them, and re-layouts  0.92 us (2%)
  waiting for transfers between devices  0.72 us (1%)
    all_to_all x2, blocking collectives, exchange(): lax.all_to_all(x, ('kv', 'm'), split_axis=0, concat_axis=0, tiled=True)  42.3 us
    pallas_call x1, Pallas kernels, shards(): pl.pallas_call(suffix_kernel, in_specs=[smem] * 2 + [vmem] * 4, out_specs...  4.84 us
    ppermute x5, starting transfers between devices, across(): return lax.ppermute(x, 'core', swap)  3.19 us
    pallas_call x1, Pallas kernels, shards(): pl.pallas_call(merge_kernel, in_specs=[smem] * 2 + [vmem] * 3, out_specs=...  1.31 us
    pallas_call x1, Pallas kernels, shards(): pl.pallas_call(combine_kernel, in_specs=[vmem], out_specs=vmem, out_shape...  1.31 us
  transfers between devices with their start and end apart: 5, of which 1 were waited for; matrix products, arithmetic and copies ran while one was open for 0% of the time, Pallas kernels for 11%

profile of v1, /device:TPU:1, one launch (start us, length us, event | category | flops | bytes accessed | tf_op | source)
XLA Modules:
  0.0 55.8 jit_solution(14411395728145859528)
XLA Ops:
  0.0 0.0 copy-start.2
  0.0 0.0 copy-start
  0.0 0.0 copy-start.1
  0.0 0.0 copy-start.4
  0.0 0.9 %copy-done.4 = bf16[2,32,128]{2,1,0:T(8,128)(2,1)S(1)} copy-done((bf16[2,32,128]{2,1,0:T(8,128)(2,1)S(1)}, bf16[2,32,128]{2,1,0:T(8,128)(2,1)}, u32[]{:S(2)}) %copy-start.4) | copy-done | bytes 16408
  0.9 0.0 copy-start.5
  0.9 0.0 copy-start.6
  0.9 0.0 copy-start.3
  0.9 24.3 %all_to_all.10.q_ref.mine_ref = bf16[64,32,128]{2,1,0:T(8,128)(2,1)S(1)} all-to-all(bf16[64,32,128]{2,1,0:T(8,128)(2,1)S(1)} %bitcast.11), channel_id=1, replica_groups=mesh['kv'=2,'m'=32,'core'=2] {'kv','m'}, dimensions={0} | all-to-all | bytes 1048576 | tf_op jit(solution)/shard_map/all_to_all | solution.py:206
  25.2 2.0 %collective-permute-start.3 = (bf16[64,32,128]{2,1,0:T(8,128)(2,1)S(1)}, bf16[64,32,128]{2,1,0:T(8,128)(2,1)S(1)}, u32[]{:S(2)}, u32[]{:S(2)}) collective-permute-start(bf16[64,32,128]{2,1,0:T(8,128)(2,1)S(1)} %all_to_all.10.q_ref.mine_ref), channel_id=1, source_target_pairs={{0,1},{1,0},{2,3},{3,2},{4,5},{5,4},{6,7},{7,6},{8,9},{9,8},{10,11... | collective-permute-start | bytes 1572872 | tf_op jit(solution)/shard_map/ppermute | solution.py:203
  27.2 0.0 copy-done.5
  27.2 0.1 collective-permute-start.1
  27.3 0.0 copy-done.6
  27.3 0.6 %collective-permute-start.2 = (bf16[4,128,128]{2,1,0:T(8,128)(2,1)S(1)}, bf16[4,128,128]{2,1,0:T(8,128)(2,1)S(1)}, u32[]{:S(2)}, u32[]{:S(2)}) collective-permute-start(bf16[4,128,128]{2,1,0:T(8,128)(2,1)S(1)} %bitcast.14), channel_id=1, source_target_pairs={{0,1},{1,0},{2,3},{3,2},{4,5},{5,4},{6,7},{7,6},{8,9},{9,8},{10,11... | collective-permute-start | bytes 393224 | tf_op jit(solution)/shard_map/ppermute | solution.py:203
  27.9 0.0 copy-done.2
  27.9 0.1 collective-permute-start
  28.0 0.7 %collective-permute-done.3.other_ref = bf16[64,32,128]{2,1,0:T(8,128)(2,1)S(1)} collective-permute-done((bf16[64,32,128]{2,1,0:T(8,128)(2,1)S(1)}, bf16[64,32,128]{2,1,0:T(8,128)(2,1)S(1)}, u32[]{:S(2)}, u32[]{:S(2)}) %collective-permute-start.3) | collective-permute-done | bytes 524320 | tf_op jit(solution)/shard_map/ppermute | solution.py:203
  28.7 0.0 copy-done
  28.7 0.0 copy-done.1
  28.7 0.0 copy-done.3
  28.7 4.8 %suffix.1.mine_ref = f32[4,40,128]{2,1,0:T(8,128)S(1)} custom-call(s32[4]{0:T(128)S(1)} %copy-done.2, s32[4]{0:T(128)S(1)} %copy-done.3, bf16[64,32,128]{2,1,0:T(8,128)(2,1)S(1)} %all_to_all.10.q_ref.mine_ref, bf16[64,32,128]{2,1,0:T(8,128)(2,1)S(1)} %collective-permute-done.3.other_ref, bf16[4,8192,128]{2,1,0:T(8,128)(2,1)S(1)} %bitcast.9, ...), custom_call_target="tpu_custom_call" | custom-call | flops 1000000000 | bytes 2097152 | tf_op jit(solution)/shard_map/suffix/pallas_call | solution.py:236
  33.6 0.5 collective-permute-start.4
  34.0 0.0 collective-permute-done.1.k1_ref
  34.0 0.0 collective-permute-done.2.v1_ref
  34.0 1.0 %prefix.1.part_ref = bf16[64,40,128]{2,1,0:T(8,128)(2,1)S(1)} custom-call(bf16[64,32,128]{2,1,0:T(8,128)(2,1)S(1)} %all_to_all.10.q_ref.mine_ref, bf16[4,128,128]{2,1,0:T(8,128)(2,1)S(1)} %bitcast.13, bf16[4,128,128]{2,1,0:T(8,128)(2,1)S(1)} %collective-permute-done.1.k1_ref, bf16[4,128,128]{2,1,0:T(8,128)(2,1)S(1)} %bitcast.15, ...), custom_call_target="tpu_custom_call" | custom-call | flops 1000000000 | bytes 2097152 | tf_op jit(solution)/shard_map/prefix/pallas_call | solution.py:226
  35.1 0.0 collective-permute-done.ids_other_ref
  35.1 0.0 collective-permute-done.4.other_ref
  35.1 1.3 %merge.1 = bf16[64,40,128]{2,1,0:T(8,128)(2,1)S(1)} custom-call(s32[4]{0:T(128)S(1)} %copy-done.2, s32[4]{0:T(128)S(1)} %collective-permute-done.ids_other_ref, bf16[64,40,128]{2,1,0:T(8,128)(2,1)S(1)} %prefix.1.part_ref, f32[4,40,128]{2,1,0:T(8,128)S(1)} %suffix.1.mine_ref, ...), custom_call_target="tpu_custom_call", output_to_operand_aliasing={{}: (2, {})} | custom-call | tf_op jit(solution)/shard_map/merge/pallas_call | solution.py:247
  36.4 18.1 %all_to_all.11.got_ref = bf16[64,40,128]{2,1,0:T(8,128)(2,1)S(1)} all-to-all(bf16[64,40,128]{2,1,0:T(8,128)(2,1)S(1)} %merge.1), channel_id=1, replica_groups=mesh['kv'=2,'m'=32,'core'=2] {'kv','m'}, dimensions={0} | all-to-all | bytes 1310720 | tf_op jit(solution)/shard_map/all_to_all | solution.py:206
  54.5 1.3 %combine.1 = bf16[2,32,128]{2,1,0:T(8,128)(2,1)} custom-call(bf16[64,40,128]{2,1,0:T(8,128)(2,1)S(1)} %all_to_all.11.got_ref), custom_call_target="tpu_custom_call" | custom-call | tf_op jit(solution)/shard_map/combine/pallas_call | solution.py:258
  (3 shorter events, 0.1 us)
Async XLA Ops:
  0.0 27.9 %copy-start.2 = (s32[4]{0:T(128)S(1)}, s32[4]{0:T(128)}, u32[]{:S(2)}) copy-start(s32[4]{0:T(128)} %ids_ref.3) | copy-start | bytes 52
  0.0 28.7 %copy-start = (bf16[4,2048,4,128]{3,2,1,0:T(4,128)(2,1)S(1)}, bf16[4,2048,4,128]{3,2,1,0:T(4,128)(2,1)}, u32[]{:S(2)}) copy-start(bf16[4,2048,4,128]{3,2,1,0:T(4,128)(2,1)} %param.10) | copy-start | bytes 25165828
  0.0 28.7 %copy-start.1 = (bf16[4,2048,4,128]{3,2,1,0:T(4,128)(2,1)S(1)}, bf16[4,2048,4,128]{3,2,1,0:T(4,128)(2,1)}, u32[]{:S(2)}) copy-start(bf16[4,2048,4,128]{3,2,1,0:T(4,128)(2,1)} %param.11) | copy-start | bytes 25165828
  0.0 0.9 %copy-start.4 = (bf16[2,32,128]{2,1,0:T(8,128)(2,1)S(1)}, bf16[2,32,128]{2,1,0:T(8,128)(2,1)}, u32[]{:S(2)}) copy-start(bf16[2,32,128]{2,1,0:T(8,128)(2,1)} %queries_ref.1) | copy-start | bytes 49156
  0.9 26.3 %copy-start.5 = (bf16[128,4,128]{2,1,0:T(4,128)(2,1)S(1)}, bf16[128,4,128]{2,1,0:T(4,128)(2,1)}, u32[]{:S(2)}) copy-start(bf16[128,4,128]{2,1,0:T(4,128)(2,1)} %param.8) | copy-start | bytes 393220
  0.9 26.4 %copy-start.6 = (bf16[128,4,128]{2,1,0:T(4,128)(2,1)S(1)}, bf16[128,4,128]{2,1,0:T(4,128)(2,1)}, u32[]{:S(2)}) copy-start(bf16[128,4,128]{2,1,0:T(4,128)(2,1)} %param.9) | copy-start | bytes 393220
  0.9 27.8 %copy-start.3 = (s32[4]{0:T(128)S(1)}, s32[4]{0:T(128)}, u32[]{:S(2)}) copy-start(s32[4]{0:T(128)} %len_ref.1) | copy-start | bytes 52
  25.2 3.5 %collective-permute-start.3 = (bf16[64,32,128]{2,1,0:T(8,128)(2,1)S(1)}, bf16[64,32,128]{2,1,0:T(8,128)(2,1)S(1)}, u32[]{:S(2)}, u32[]{:S(2)}) collective-permute-start(bf16[64,32,128]{2,1,0:T(8,128)(2,1)S(1)} %all_to_all.10.q_ref.mine_ref), channel_id=1, source_target_pairs={{0,1},{1,0},{2,3},{3,2},{4,5},{5,4},{6,7},{7,6},{8,9},{9,8},{10,11... | collective-permute-start | bytes 1572872 | tf_op jit(solution)/shard_map/ppermute | solution.py:203
  27.2 6.8 %collective-permute-start.1 = (bf16[4,128,128]{2,1,0:T(8,128)(2,1)S(1)}, bf16[4,128,128]{2,1,0:T(8,128)(2,1)S(1)}, u32[]{:S(2)}, u32[]{:S(2)}) collective-permute-start(bf16[4,128,128]{2,1,0:T(8,128)(2,1)S(1)} %bitcast.12), channel_id=1, source_target_pairs={{0,1},{1,0},{2,3},{3,2},{4,5},{5,4},{6,7},{7,6},{8,9},{9,8},{10,11... | collective-permute-start | bytes 393224 | tf_op jit(solution)/shard_map/ppermute | solution.py:203
  27.3 6.7 %collective-permute-start.2 = (bf16[4,128,128]{2,1,0:T(8,128)(2,1)S(1)}, bf16[4,128,128]{2,1,0:T(8,128)(2,1)S(1)}, u32[]{:S(2)}, u32[]{:S(2)}) collective-permute-start(bf16[4,128,128]{2,1,0:T(8,128)(2,1)S(1)} %bitcast.14), channel_id=1, source_target_pairs={{0,1},{1,0},{2,3},{3,2},{4,5},{5,4},{6,7},{7,6},{8,9},{9,8},{10,11... | collective-permute-start | bytes 393224 | tf_op jit(solution)/shard_map/ppermute | solution.py:203
  27.9 7.2 %collective-permute-start = (s32[4]{0:T(128)S(1)}, s32[4]{0:T(128)S(1)}, u32[]{:S(2)}, u32[]{:S(2)}) collective-permute-start(s32[4]{0:T(128)S(1)} %copy-done.2), channel_id=1, source_target_pairs={{0,1},{1,0},{2,3},{3,2},{4,5},{5,4},{6,7},{7,6},{8,9},{9,8},{10,11... | collective-permute-start | bytes 56 | tf_op jit(solution)/shard_map/ppermute | solution.py:203
  33.6 1.5 %collective-permute-start.4 = (f32[4,40,128]{2,1,0:T(8,128)S(1)}, f32[4,40,128]{2,1,0:T(8,128)S(1)}, u32[]{:S(2)}, u32[]{:S(2)}) collective-permute-start(f32[4,40,128]{2,1,0:T(8,128)S(1)} %suffix.1.mine_ref), channel_id=1, source_target_pairs={{0,1},{1,0},{2,3},{3,2},{4,5},{5,4},{6,7},{7,6},{8,9},{9,8},{10,11... | collective-permute-start | bytes 245768 | tf_op jit(solution)/shard_map/ppermute | solution.py:203

commit v2 on v1

v2 whole, which is shorter than its diff:
```python
import jax
import jax.numpy as jnp
from jax import lax
from jax.experimental import pallas as pl
from jax.experimental.pallas import tpu as pltpu
from jax.sharding import Mesh
from jax.sharding import PartitionSpec as P

negative_fill = -1e30
f32 = jnp.float32
bf16 = jnp.bfloat16
in_hbm = pl.BlockSpec(memory_space=pltpu.HBM)
vmem = pl.BlockSpec(memory_space=pltpu.VMEM)


def limit(mib):
    return pltpu.CompilerParams(vmem_limit_bytes=mib << 20)


def rounded(x):
    return x.astype(bf16).astype(f32)


def nt_dot(a, b):
    return lax.dot_general(a, b, (((1,), (1,)), ((), ())), preferred_element_type=f32)


def ask_kernel(queries_ref, out_ref):
    groups, copies = out_ref.shape[:2]
    sub8 = lax.broadcasted_iota(jnp.int32, (8, out_ref.shape[3]), 0)
    for g in range(groups):
        tiles = []
        for k in (0, 2):
            base = 16 * g + 4 * k
            one = queries_ref[0, base : base + 8, :].astype(f32)
            two = queries_ref[1, base : base + 8, :].astype(f32)
            tiles.append(jnp.where(sub8 < 4, one, pltpu.roll(two, 4, 0)))
            tiles.append(jnp.where(sub8 < 4, pltpu.roll(one, 4, 0), two))
        piece = jnp.concatenate(tiles, axis=0).astype(bf16)
        for c in range(copies):
            out_ref[g, c] = piece


def prefix_kernel(q_ref, k0_ref, v0_ref, k1_ref, v1_ref, out_ref, wide_ref):
    pieces = q_ref.shape[0]
    positions, kv_local, dim = k0_ref.shape
    scale = dim ** (-0.5)
    rows = pieces * 8
    lane = lax.broadcasted_iota(jnp.int32, (rows, 128), 1)
    stat = jnp.zeros((rows, 128), f32)
    for n, pair in enumerate(((k0_ref, k1_ref), (v0_ref, v1_ref))):
        for c, ref in enumerate(pair):
            wide_ref[n, c] = ref[...].astype(f32).reshape(positions * kv_local, dim)

    def block(n, k):
        parts = [wide_ref[n, c, pl.ds(k, positions, stride=kv_local), :] for c in range(2)]
        return jnp.concatenate(parts, axis=0).astype(bf16)

    for k in range(kv_local):
        q = q_ref[:, 8 * k : 8 * k + 8, :].astype(f32).reshape(rows, dim).astype(bf16)
        keys, values = block(0, k), block(1, k)
        scores = nt_dot(q, keys) * scale
        best = rounded(jnp.max(scores, axis=1, keepdims=True))
        weights = jnp.exp(scores - best)
        total = jnp.sum(weights, axis=1, keepdims=True)
        acc = jnp.dot(weights.astype(bf16), values, preferred_element_type=f32)
        out_ref[:, 8 * k : 8 * k + 8, :] = acc.reshape(pieces, 8, dim).astype(bf16)
        high = rounded(total)
        stat = jnp.where(lane == 4 * k, best, stat)
        stat = jnp.where(lane == 4 * k + 1, high, stat)
        stat = jnp.where(lane == 4 * k + 2, total - high, stat)
    out_ref[:, 8 * kv_local : 8 * kv_local + 8, :] = stat.reshape(pieces, 8, 128).astype(bf16)


def place_of(sequence):
    device = sequence // 2
    return device // 2, device % 2, sequence % 2


def scalars_of(ref):
    row = ref[...]
    return [row[0, n] for n in range(row.shape[1])]


def tile_of(x, k, i):
    x = x[8 * (k // 2) : 8 * (k // 2) + 8]
    return jnp.where(i == k % 2, x, pltpu.roll(x, 4, 0))


def merged(old_stat, old_acc, best_new, total_new, acc_new, used, lane8):
    stat, accs = old_stat, []
    for k in range(4):
        best_old, high, low = (old_stat[:, 4 * k + c : 4 * k + c + 1] for c in range(3))
        best = jnp.maximum(best_old, best_new[k])
        first = jnp.exp(best_old - best)
        second = jnp.exp(best_new[k] - best)
        total = (high + low) * first + total_new[k] * second
        accs.append(jnp.where(used, old_acc[k] * first + acc_new[k] * second, old_acc[k]))
        rest = rounded(total)
        stat = jnp.where(used & (lane8 == 4 * k), best, stat)
        stat = jnp.where(used & (lane8 == 4 * k + 1), rest, stat)
        stat = jnp.where(used & (lane8 == 4 * k + 2), total - rest, stat)
    return stat, accs


def part_at(ref, piece):
    return ref[piece, 32:40, :].astype(f32), [
        ref[piece, 8 * k : 8 * k + 8, :].astype(f32) for k in range(4)
    ]


def suffix_kernel(
    ids_ref, len_ref, mine_ref, other_ref, keys_ref, values_ref, part_ref, out_ref, found_ref
):
    del part_ref
    slots, wide, dim = keys_ref.shape
    scale = dim ** (-0.5)
    log2e = 1.4426950408889634
    chunk = 1024
    row = lax.broadcasted_iota(jnp.int32, (16, chunk), 0)
    lane = lax.broadcasted_iota(jnp.int32, (16, chunk), 1)
    position = jnp.where(lane % 4 == row // 4, lane // 4, 1 << 20)
    sub8 = lax.broadcasted_iota(jnp.int32, (8, dim), 0)
    lane8 = lax.broadcasted_iota(jnp.int32, (8, dim), 1)
    my_core = lax.axis_index("core")
    ids, lengths = scalars_of(ids_ref), scalars_of(len_ref)

    def scores_of(s):
        piece, core, i = place_of(ids[s])
        length = lengths[s]
        q = jnp.where(core == my_core, mine_ref[piece].astype(f32), other_ref[piece].astype(f32))
        pairs = []
        for k in (0, 2):
            even, odd = q[8 * k : 8 * k + 8], q[8 * k + 8 : 8 * k + 16]
            even = jnp.where(i == 0, even, pltpu.roll(even, 4, 0))
            odd = jnp.where(i == 0, pltpu.roll(odd, 4, 0), odd)
            pairs.append(jnp.where(sub8 < 4, even, odd))
        q16 = jnp.concatenate(pairs, axis=0).astype(bf16)
        parts = []
        peak = jnp.full((16, 128), negative_fill, f32)
        for c in range(wide // chunk):
            part = nt_dot(q16, keys_ref[s, c * chunk : (c + 1) * chunk, :])
            part = jnp.where(position < length - c * (chunk // 4), part, negative_fill)
            for t in range(chunk // 128):
                peak = jnp.maximum(peak, part[:, 128 * t : 128 * t + 128])
            parts.append(part)
        return parts, rounded(jnp.max(peak, axis=1, keepdims=True) * scale)

    def finish(s, parts, best):
        sums = jnp.zeros((16, 128), f32)
        acc = jnp.zeros((16, dim), f32)
        for c in range(wide // chunk):
            weights = jnp.exp2(parts[c] * (scale * log2e) - best * log2e)
            for t in range(chunk // 128):
                sums = sums + weights[:, 128 * t : 128 * t + 128]
            acc = acc + jnp.dot(
                weights.astype(bf16),
                values_ref[s, c * chunk : (c + 1) * chunk, :],
                preferred_element_type=f32,
            )
        total = jnp.broadcast_to(jnp.sum(sums, axis=1, keepdims=True), (16, dim))
        best = jnp.broadcast_to(best, (16, dim))
        piece, core, i = place_of(ids[s])
        bests, totals, accs = ([tile_of(x, k, i) for k in range(4)] for x in (best, total, acc))
        stat = jnp.zeros((8, dim), f32)
        for k in range(4):
            found_ref[s, 8 * k : 8 * k + 8, :] = accs[k]
            stat = jnp.where(lane8 == 4 * k, bests[k], stat)
            stat = jnp.where(lane8 == 4 * k + 1, totals[k], stat)
        found_ref[s, 32:40, :] = jnp.where(lane8 == 16, ids[s].astype(f32), stat)
        used = (sub8 // 4 == i) & (core == my_core)
        old_stat, old_accs = part_at(out_ref, piece)
        stat, accs = merged(old_stat, old_accs, bests, totals, accs, used, lane8)
        for k in range(4):
            out_ref[piece, 8 * k : 8 * k + 8, :] = accs[k].astype(bf16)
        out_ref[piece, 32:40, :] = stat.astype(bf16)

    ready = scores_of(0)
    for s in range(slots):
        following = scores_of(s + 1) if s + 1 < slots else None
        finish(s, *ready)
        ready = following


def merge_kernel(part_ref, found_ref, out_ref):
    del part_ref
    sub8 = lax.broadcasted_iota(jnp.int32, (8, 128), 0)
    lane8 = lax.broadcasted_iota(jnp.int32, (8, 128), 1)
    results = []
    places = []
    for s in range(found_ref.shape[0]):
        new = found_ref[s, 32:40, :]
        piece, core, i = place_of(new[0, 16].astype(jnp.int32))
        places.append((piece, core))
        bests, totals = ([new[:, 4 * k + c : 4 * k + c + 1] for k in range(4)] for c in range(2))
        accs = [found_ref[s, 8 * k : 8 * k + 8, :] for k in range(4)]
        old_stat, old_accs = part_at(out_ref, piece)
        results.append(merged(old_stat, old_accs, bests, totals, accs, sub8 // 4 == i, lane8))
    for s, (stat, accs) in enumerate(results):
        piece, core = places[s]

        @pl.when(core == lax.axis_index("core"))
        def _():
            for k in range(4):
                out_ref[piece, 8 * k : 8 * k + 8, :] = accs[k].astype(bf16)
            out_ref[piece, 32:40, :] = stat.astype(bf16)


def combine_kernel(got_ref, out_hbm, out_ref, sems):
    copies = []
    count = got_ref.shape[0] // 2
    sub8 = lax.broadcasted_iota(jnp.int32, (8, 128), 0)
    for half in range(2):
        at = slice(half * count, (half + 1) * count)
        stat = got_ref[at, 32:40, :].astype(f32)
        top = jnp.max(stat, axis=0, keepdims=True)
        factor = jnp.exp(stat - top)
        total = pltpu.roll(stat, 127, 2) + pltpu.roll(stat, 126, 2)
        factor = factor / jnp.sum(factor * total, axis=0, keepdims=True)
        rows = []
        for k in range(4):
            acc = got_ref[at, 8 * k : 8 * k + 8, :].astype(f32)
            rows.append(jnp.sum(acc * factor[:, :, 4 * k : 4 * k + 1], axis=0))
        for k in (0, 2):
            base = 16 * half + 4 * k
            turned = pltpu.roll(rows[k + 1], 4, 0)
            out_ref[0, base : base + 8, :] = jnp.where(sub8 < 4, rows[k], turned).astype(bf16)
            turned = pltpu.roll(rows[k], 4, 0)
            out_ref[1, base : base + 8, :] = jnp.where(sub8 < 4, turned, rows[k + 1]).astype(bf16)
        part = (slice(None), slice(16 * half, 16 * half + 16))
        copies.append(pltpu.make_async_copy(out_ref.at[part], out_hbm.at[part], sems.at[half]))
        copies[half].start()
    for copy in copies:
        copy.wait()


def shards(
    queries, prefix_keys, prefix_values, suffix_keys, suffix_values, suffix_lengths, slot_sequence
):
    kv_count = lax.axis_size("kv")
    m_count = lax.axis_size("m")
    per_device, head_count, dim = queries.shape
    local_heads = head_count // kv_count
    kv_local = prefix_keys.shape[1]
    pieces = kv_count * m_count
    slots, suffix_len = suffix_keys.shape[:2]
    swap = [(0, 1), (1, 0)]

    def across(x):
        return lax.ppermute(x, "core", swap)

    def exchange(x):
        return lax.all_to_all(x, ("kv", "m"), split_axis=0, concat_axis=0, tiled=True)

    sent = pl.pallas_call(
        ask_kernel,
        in_specs=[vmem],
        out_specs=vmem,
        out_shape=jax.ShapeDtypeStruct((kv_count, m_count, per_device * local_heads, dim), bf16),
        cost_estimate=pl.CostEstimate(flops=10**11, transcendentals=0, bytes_accessed=2**28),
        compiler_params=limit(4),
        name="ask",
    )(queries)
    there = across(prefix_keys), across(prefix_values)
    mine = exchange(sent.reshape(pieces, per_device * local_heads, dim))
    other = across(mine)

    part = pl.pallas_call(
        prefix_kernel,
        in_specs=[vmem] * 5,
        out_specs=vmem,
        out_shape=jax.ShapeDtypeStruct((pieces, per_device * local_heads + 8, dim), bf16),
        cost_estimate=pl.CostEstimate(flops=10**9, transcendentals=0, bytes_accessed=2**21),
        scratch_shapes=[pltpu.VMEM((2, 2, prefix_keys.shape[0] * kv_local, dim), f32)],
        compiler_params=limit(6),
        name="prefix",
    )(mine, prefix_keys, prefix_values, *there)

    keys = suffix_keys.reshape(slots, suffix_len * kv_local, dim)
    values = suffix_values.reshape(slots, suffix_len * kv_local, dim)
    part, found = pl.pallas_call(
        suffix_kernel,
        in_specs=[vmem] * 7,
        out_specs=[vmem] * 2,
        out_shape=[
            jax.ShapeDtypeStruct(part.shape, bf16),
            jax.ShapeDtypeStruct((slots, per_device * local_heads + 8, dim), f32),
        ],
        input_output_aliases={6: 0},
        cost_estimate=pl.CostEstimate(flops=10**9, transcendentals=0, bytes_accessed=2**21),
        compiler_params=limit(4),
        name="suffix",
    )(*(x.reshape(1, slots) for x in (slot_sequence, suffix_lengths)), mine, other, keys, values, part)
    found_there = across(found)

    part = pl.pallas_call(
        merge_kernel,
        in_specs=[vmem] * 2,
        out_specs=vmem,
        out_shape=jax.ShapeDtypeStruct(part.shape, bf16),
        input_output_aliases={0: 0},
        compiler_params=limit(4),
        name="merge",
    )(part, found_there)

    got = exchange(part)
    return pl.pallas_call(
        combine_kernel,
        in_specs=[vmem],
        out_specs=in_hbm,
        out_shape=jax.ShapeDtypeStruct(queries.shape, bf16),
        scratch_shapes=[pltpu.VMEM(queries.shape, bf16), pltpu.SemaphoreType.DMA((2,))],
        compiler_params=limit(4),
        name="combine",
    )(got)


def solution(mesh):
    kv, batch = (mesh.shape[a] for a in ("kv", "batch"))
    fine = Mesh(mesh.devices.reshape(kv, batch // 2, 2), ("kv", "m", "core"))
    rows, positions = ("kv", "m", "core"), ("m", "core")
    return jax.shard_map(
        shards,
        mesh=fine,
        in_specs=(
            P(rows, None, None),
            P(positions, "kv", None),
            P(positions, "kv", None),
            P(positions, None, "kv", None),
            P(positions, None, "kv", None),
            P(positions),
            P(positions),
        ),
        out_specs=P(rows, None, None),
        check_vma=False,
    )
```

time: 56.5 us -> 55.8 us (0.988)
  Pallas kernels: 8.53 us -> 6.64 us
  waiting for transfers between devices: 0.72 us -> 2.32 us
    pallas_call x3, Pallas kernels: 7.45 us -> 5.5 us  [the longest x1 3.81 us: shards(): pl.pallas_call(suffix_kernel, in_specs=[vmem] * 7, out_specs=[vmem] * 2,...]
    ppermute x5 -> x4, waiting for transfers between devices: 0.72 us -> 2.32 us  [across(): return lax.ppermute(x, 'core', swap)]
    ppermute x5 -> x4, starting transfers between devices: 3.19 us -> 2.95 us  [across(): return lax.ppermute(x, 'core', swap)]
  transfers between devices with their start and end apart: 5 -> 4, of which waited for: 1 -> 3; matrix products, arithmetic and copies ran while one was open for 0% -> 0% of each run, Pallas kernels for 11% -> 2%
where the time goes in v2:
time: 55.8 us; the launch traced here: 54.9 us
  blocking collectives  42.2 us (76%)
  Pallas kernels  6.64 us (12%)
  starting transfers between devices  2.95 us (5%)
  waiting for transfers between devices  2.32 us (4%)
  local copies, waits for them, and re-layouts  0.77 us (1%)
    all_to_all x2, blocking collectives, exchange(): lax.all_to_all(x, ('kv', 'm'), split_axis=0, concat_axis=0, tiled=True)  42.2 us
    pallas_call x1, Pallas kernels, shards(): pl.pallas_call(suffix_kernel, in_specs=[vmem] * 7, out_specs=[vmem] * 2,...  3.81 us
    ppermute x4, starting transfers between devices, across(): return lax.ppermute(x, 'core', swap)  2.95 us
    ppermute x4, waiting for transfers between devices, across(): return lax.ppermute(x, 'core', swap)  2.32 us
    pallas_call x1, Pallas kernels, shards(): pl.pallas_call(combine_kernel, in_specs=[vmem], out_specs=in_hbm, out_sha...  1.32 us
  transfers between devices with their start and end apart: 4, of which 3 were waited for; matrix products, arithmetic and copies ran while one was open for 0% of the time, Pallas kernels for 2%

profile of v2, /device:TPU:1, one launch (start us, length us, event | category | flops | bytes accessed | tf_op | source)
XLA Modules:
  0.0 54.9 jit_solution(12040255138068278483)
XLA Ops:
  0.0 0.0 copy-start.4
  0.0 0.0 copy-start.5
  0.0 0.0 copy-start.2
  0.0 0.0 copy-start.3
  0.0 0.0 copy-start.6
  0.0 0.8 %copy-done.6 = bf16[2,32,128]{2,1,0:T(8,128)(2,1)S(1)} copy-done((bf16[2,32,128]{2,1,0:T(8,128)(2,1)S(1)}, bf16[2,32,128]{2,1,0:T(8,128)(2,1)}, u32[]{:S(2)}) %copy-start.6) | copy-done | bytes 16408
  0.8 0.0 copy-start
  0.8 0.0 copy-start.1
  0.8 24.3 %all_to_all.10.q_ref.mine_ref = bf16[64,32,128]{2,1,0:T(8,128)(2,1)S(1)} all-to-all(bf16[64,32,128]{2,1,0:T(8,128)(2,1)S(1)} %bitcast.7), channel_id=1, replica_groups=mesh['kv'=2,'m'=32,'core'=2] {'kv','m'}, dimensions={0} | all-to-all | bytes 1048576 | tf_op jit(solution)/shard_map/all_to_all | solution.py:253
  25.1 2.0 %collective-permute-start = (bf16[64,32,128]{2,1,0:T(8,128)(2,1)S(1)}, bf16[64,32,128]{2,1,0:T(8,128)(2,1)S(1)}, u32[]{:S(2)}, u32[]{:S(2)}) collective-permute-start(bf16[64,32,128]{2,1,0:T(8,128)(2,1)S(1)} %all_to_all.10.q_ref.mine_ref), channel_id=1, source_target_pairs={{0,1},{1,0},{2,3},{3,2},{4,5},{5,4},{6,7},{7,6},{8,9},{9,8},{10,11... | collective-permute-start | bytes 1572872 | tf_op jit(solution)/shard_map/ppermute | solution.py:250
  27.1 0.0 copy-done.4
  27.1 0.0 collective-permute-start.1
  27.1 0.0 copy-done.5
  27.1 0.5 collective-permute-start.2
  27.6 1.2 %collective-permute-done.1.k1_ref = bf16[128,4,128]{2,1,0:T(4,128)(2,1)S(1)} collective-permute-done((bf16[128,4,128]{2,1,0:T(4,128)(2,1)S(1)}, bf16[128,4,128]{2,1,0:T(4,128)(2,1)S(1)}, u32[]{:S(2)}, u32[]{:S(2)}) %collective-permute-start.1) | collective-permute-done | bytes 131104 | tf_op jit(solution)/shard_map/ppermute | solution.py:250
  28.8 0.2 collective-permute-done.2.v1_ref
  29.0 1.1 %prefix.1.part_ref = bf16[64,40,128]{2,1,0:T(8,128)(2,1)S(1)} custom-call(bf16[64,32,128]{2,1,0:T(8,128)(2,1)S(1)} %all_to_all.10.q_ref.mine_ref, bf16[128,4,128]{2,1,0:T(4,128)(2,1)S(1)} %copy-done.4, bf16[128,4,128]{2,1,0:T(4,128)(2,1)S(1)} %copy-done.5, bf16[128,4,128]{2,1,0:T(4,128)(2,1)S(1)} %collective-permute-done.1.k1_ref, ...), custom_call_target="tpu_custom_call" | custom-call | flops 1000000000 | bytes 2097152 | tf_op jit(solution)/shard_map/prefix/pallas_call | solution.py:268
  30.1 0.0 collective-permute-done.other_ref
  30.1 0.0 copy-done.2
  30.1 0.0 copy-done.3
  30.1 0.0 copy-done
  30.1 0.0 copy-done.1
  30.1 3.8 %suffix.1 = (bf16[64,40,128]{2,1,0:T(8,128)(2,1)S(1)}, f32[4,40,128]{2,1,0:T(8,128)S(1)}) custom-call(s32[1,4]{1,0:T(1,128)S(1)} %bitcast.8, s32[1,4]{1,0:T(1,128)S(1)} %bitcast.9, bf16[64,32,128]{2,1,0:T(8,128)(2,1)S(1)} %all_to_all.10.q_ref.mine_ref, bf16[64,32,128]{2,1,0:T(8,128)(2,1)S(1)} %collective-permute-done.other_ref, ...), custom_call_target="tpu_custom_call", output_to_operand_aliasing={{0}: (6, {})} | custom-call | flops 1000000000 | bytes 2097152 | tf_op jit(solution)/shard_map/suffix/pallas_call | solution.py:281
  34.0 0.5 collective-permute-start.3
  34.4 0.9 %collective-permute-done.3.found_ref = f32[4,40,128]{2,1,0:T(8,128)S(1)} collective-permute-done((f32[4,40,128]{2,1,0:T(8,128)S(1)}, f32[4,40,128]{2,1,0:T(8,128)S(1)}, u32[]{:S(2)}, u32[]{:S(2)}) %collective-permute-start.3) | collective-permute-done | bytes 81952 | tf_op jit(solution)/shard_map/ppermute | solution.py:250
  35.3 0.4 merge.1
  35.7 17.9 %all_to_all.11.got_ref = bf16[64,40,128]{2,1,0:T(8,128)(2,1)S(1)} all-to-all(bf16[64,40,128]{2,1,0:T(8,128)(2,1)S(1)} %merge.1), channel_id=1, replica_groups=mesh['kv'=2,'m'=32,'core'=2] {'kv','m'}, dimensions={0} | all-to-all | bytes 1310720 | tf_op jit(solution)/shard_map/all_to_all | solution.py:253
  53.6 1.3 %combine.1 = bf16[2,32,128]{2,1,0:T(8,128)(2,1)} custom-call(bf16[64,40,128]{2,1,0:T(8,128)(2,1)S(1)} %all_to_all.11.got_ref), custom_call_target="tpu_custom_call" | custom-call | tf_op jit(solution)/shard_map/combine/pallas_call | solution.py:307
  (1 shorter events, 0.0 us)
Async XLA Ops:
  0.0 27.1 %copy-start.4 = (bf16[128,4,128]{2,1,0:T(4,128)(2,1)S(1)}, bf16[128,4,128]{2,1,0:T(4,128)(2,1)}, u32[]{:S(2)}) copy-start(bf16[128,4,128]{2,1,0:T(4,128)(2,1)} %k0_ref.1) | copy-start | bytes 393220
  0.0 27.1 %copy-start.5 = (bf16[128,4,128]{2,1,0:T(4,128)(2,1)S(1)}, bf16[128,4,128]{2,1,0:T(4,128)(2,1)}, u32[]{:S(2)}) copy-start(bf16[128,4,128]{2,1,0:T(4,128)(2,1)} %v0_ref.1) | copy-start | bytes 393220
  0.0 30.1 %copy-start.2 = (s32[4]{0:T(128)S(1)}, s32[4]{0:T(128)}, u32[]{:S(2)}) copy-start(s32[4]{0:T(128)} %param.13) | copy-start | bytes 52
  0.0 30.1 %copy-start.3 = (s32[4]{0:T(128)S(1)}, s32[4]{0:T(128)}, u32[]{:S(2)}) copy-start(s32[4]{0:T(128)} %param.12) | copy-start | bytes 52
  0.0 0.8 %copy-start.6 = (bf16[2,32,128]{2,1,0:T(8,128)(2,1)S(1)}, bf16[2,32,128]{2,1,0:T(8,128)(2,1)}, u32[]{:S(2)}) copy-start(bf16[2,32,128]{2,1,0:T(8,128)(2,1)} %queries_ref.1) | copy-start | bytes 49156
  0.8 29.3 %copy-start = (bf16[4,2048,4,128]{3,2,1,0:T(4,128)(2,1)S(1)}, bf16[4,2048,4,128]{3,2,1,0:T(4,128)(2,1)}, u32[]{:S(2)}) copy-start(bf16[4,2048,4,128]{3,2,1,0:T(4,128)(2,1)} %param.10) | copy-start | bytes 25165828
  0.8 29.4 %copy-start.1 = (bf16[4,2048,4,128]{3,2,1,0:T(4,128)(2,1)S(1)}, bf16[4,2048,4,128]{3,2,1,0:T(4,128)(2,1)}, u32[]{:S(2)}) copy-start(bf16[4,2048,4,128]{3,2,1,0:T(4,128)(2,1)} %param.11) | copy-start | bytes 25165828
  25.1 5.0 %collective-permute-start = (bf16[64,32,128]{2,1,0:T(8,128)(2,1)S(1)}, bf16[64,32,128]{2,1,0:T(8,128)(2,1)S(1)}, u32[]{:S(2)}, u32[]{:S(2)}) collective-permute-start(bf16[64,32,128]{2,1,0:T(8,128)(2,1)S(1)} %all_to_all.10.q_ref.mine_ref), channel_id=1, source_target_pairs={{0,1},{1,0},{2,3},{3,2},{4,5},{5,4},{6,7},{7,6},{8,9},{9,8},{10,11... | collective-permute-start | bytes 1572872 | tf_op jit(solution)/shard_map/ppermute | solution.py:250
  27.1 1.7 %collective-permute-start.1 = (bf16[128,4,128]{2,1,0:T(4,128)(2,1)S(1)}, bf16[128,4,128]{2,1,0:T(4,128)(2,1)S(1)}, u32[]{:S(2)}, u32[]{:S(2)}) collective-permute-start(bf16[128,4,128]{2,1,0:T(4,128)(2,1)S(1)} %copy-done.4), channel_id=1, source_target_pairs={{0,1},{1,0},{2,3},{3,2},{4,5},{5,4},{6,7},{7,6},{8,9},{9,8},{10,11... | collective-permute-start | bytes 393224 | tf_op jit(solution)/shard_map/ppermute | solution.py:250
  27.1 1.9 %collective-permute-start.2 = (bf16[128,4,128]{2,1,0:T(4,128)(2,1)S(1)}, bf16[128,4,128]{2,1,0:T(4,128)(2,1)S(1)}, u32[]{:S(2)}, u32[]{:S(2)}) collective-permute-start(bf16[128,4,128]{2,1,0:T(4,128)(2,1)S(1)} %copy-done.5), channel_id=1, source_target_pairs={{0,1},{1,0},{2,3},{3,2},{4,5},{5,4},{6,7},{7,6},{8,9},{9,8},{10,11... | collective-permute-start | bytes 393224 | tf_op jit(solution)/shard_map/ppermute | solution.py:250
  34.0 1.4 %collective-permute-start.3 = (f32[4,40,128]{2,1,0:T(8,128)S(1)}, f32[4,40,128]{2,1,0:T(8,128)S(1)}, u32[]{:S(2)}, u32[]{:S(2)}) collective-permute-start(f32[4,40,128]{2,1,0:T(8,128)S(1)} %get-tuple-element.8), channel_id=1, source_target_pairs={{0,1},{1,0},{2,3},{3,2},{4,5},{5,4},{6,7},{7,6},{8,9},{9,8},{10,11... | collective-permute-start | bytes 245768 | tf_op jit(solution)/shard_map/ppermute | solution.py:250

commit v3 on v2

v3 whole, which is shorter than its diff:
```python
import jax
import jax.numpy as jnp
from jax import lax
from jax.experimental import pallas as pl
from jax.experimental.pallas import tpu as pltpu
from jax.sharding import Mesh
from jax.sharding import PartitionSpec as P

negative_fill = -1e30
f32 = jnp.float32
bf16 = jnp.bfloat16
vmem = pl.BlockSpec(memory_space=pltpu.VMEM)


def limit(mib):
    return pltpu.CompilerParams(vmem_limit_bytes=mib << 20)


def rounded(x):
    return x.astype(bf16).astype(f32)


def nt_dot(a, b):
    return lax.dot_general(a, b, (((1,), (1,)), ((), ())), preferred_element_type=f32)


def scalars_of(ref):
    row = ref[...]
    return [row[0, n] for n in range(row.shape[1])]


def ask_kernel(queries_ref, out_ref):
    groups, copies = out_ref.shape[:2]
    sub8 = lax.broadcasted_iota(jnp.int32, (8, out_ref.shape[3]), 0)
    for g in range(groups):
        tiles = []
        for k in (0, 2):
            base = 16 * g + 4 * k
            one = queries_ref[0, base : base + 8, :].astype(f32)
            two = queries_ref[1, base : base + 8, :].astype(f32)
            tiles.append(jnp.where(sub8 < 4, one, pltpu.roll(two, 4, 0)))
            tiles.append(jnp.where(sub8 < 4, pltpu.roll(one, 4, 0), two))
        piece = jnp.concatenate(tiles, axis=0).astype(bf16)
        for c in range(copies):
            out_ref[g, c] = piece


def stat_with(stat, lane, k, best, total):
    high = rounded(total)
    stat = jnp.where(lane == 4 * k, best, stat)
    stat = jnp.where(lane == 4 * k + 1, high, stat)
    return jnp.where(lane == 4 * k + 2, total - high, stat)


def prefix_kernel(q_ref, k0_ref, v0_ref, k1_ref, v1_ref, out_ref, wide_ref):
    pieces = q_ref.shape[0]
    positions, kv_local, dim = k0_ref.shape
    scale = dim ** (-0.5)
    rows = pieces * 8
    lane = lax.broadcasted_iota(jnp.int32, (rows, 128), 1)
    stat = jnp.zeros((rows, 128), f32)
    for n, pair in enumerate(((k0_ref, k1_ref), (v0_ref, v1_ref))):
        for c, ref in enumerate(pair):
            wide_ref[n, c] = ref[...].astype(f32).reshape(positions * kv_local, dim)

    def block_of(n, k):
        parts = [wide_ref[n, c, pl.ds(k, positions, stride=kv_local), :] for c in range(2)]
        return jnp.concatenate(parts, axis=0).astype(bf16)

    for k in range(kv_local):
        q = q_ref[:, 8 * k : 8 * k + 8, :].astype(f32).reshape(rows, dim).astype(bf16)
        keys, values = block_of(0, k), block_of(1, k)
        scores = nt_dot(q, keys) * scale
        best = rounded(jnp.max(scores, axis=1, keepdims=True))
        weights = jnp.exp(scores - best)
        total = jnp.sum(weights, axis=1, keepdims=True)
        acc = jnp.dot(weights.astype(bf16), values, preferred_element_type=f32)
        out_ref[:, 8 * k : 8 * k + 8, :] = acc.reshape(pieces, 8, dim).astype(bf16)
        stat = stat_with(stat, lane, k, best, total)
    out_ref[:, 8 * kv_local : 8 * kv_local + 8, :] = stat.reshape(pieces, 8, 128).astype(bf16)


def place_of(sequence):
    device = sequence // 2
    return device // 2, device % 2, sequence % 2


def tile_of(x, k, i):
    x = x[8 * (k // 2) : 8 * (k // 2) + 8]
    return jnp.where(i == k % 2, x, pltpu.roll(x, 4, 0))


def merged(piece_ref, piece, new, used):
    lane = lax.broadcasted_iota(jnp.int32, (8, 128), 1)
    old_stat, new_stat = piece_ref[piece, 32:40, :].astype(f32), new[32:40]
    stat, tiles = jnp.zeros((8, 128), f32), []
    for k in range(4):
        at = slice(8 * k, 8 * k + 8)
        best_old, high, low = (old_stat[:, 4 * k + c : 4 * k + c + 1] for c in range(3))
        best_new, total_new = (new_stat[:, 4 * k + c : 4 * k + c + 1] for c in range(2))
        best = jnp.maximum(best_old, best_new)
        first, second = jnp.exp(best_old - best), jnp.exp(best_new - best)
        old = piece_ref[piece, at, :].astype(f32)
        tiles.append(jnp.where(used, old * first + new[at] * second, old))
        stat = stat_with(stat, lane, k, best, (high + low) * first + total_new * second)
    return [*tiles, jnp.where(used, stat, old_stat)]


def suffix_kernel(ids_ref, len_ref, mine_ref, other_ref, keys_ref, values_ref, found_ref):
    slots, wide, dim = keys_ref.shape
    scale = dim ** (-0.5)
    log2e = 1.4426950408889634
    chunk = 1024
    row = lax.broadcasted_iota(jnp.int32, (16, chunk), 0)
    lane = lax.broadcasted_iota(jnp.int32, (16, chunk), 1)
    position = jnp.where(lane % 4 == row // 4, lane // 4, 1 << 20)
    sub8 = lax.broadcasted_iota(jnp.int32, (8, dim), 0)
    lane8 = lax.broadcasted_iota(jnp.int32, (8, dim), 1)
    my_core = lax.axis_index("core")
    ids, lengths = scalars_of(ids_ref), scalars_of(len_ref)

    def scores_of(s):
        piece, core, i = place_of(ids[s])
        length = lengths[s]
        q = jnp.where(core == my_core, mine_ref[piece].astype(f32), other_ref[piece].astype(f32))
        pairs = []
        for k in (0, 2):
            even, odd = q[8 * k : 8 * k + 8], q[8 * k + 8 : 8 * k + 16]
            even = jnp.where(i == 0, even, pltpu.roll(even, 4, 0))
            odd = jnp.where(i == 0, pltpu.roll(odd, 4, 0), odd)
            pairs.append(jnp.where(sub8 < 4, even, odd))
        q16 = jnp.concatenate(pairs, axis=0).astype(bf16)
        parts = []
        peak = jnp.full((16, 128), negative_fill, f32)
        for c in range(wide // chunk):
            part = nt_dot(q16, keys_ref[s, c * chunk : (c + 1) * chunk, :])
            part = jnp.where(position < length - c * (chunk // 4), part, negative_fill)
            for t in range(chunk // 128):
                peak = jnp.maximum(peak, part[:, 128 * t : 128 * t + 128])
            parts.append(part)
        return parts, rounded(jnp.max(peak, axis=1, keepdims=True) * scale)

    def finish(s, parts, best):
        sums = jnp.zeros((16, 128), f32)
        acc = jnp.zeros((16, dim), f32)
        for c in range(wide // chunk):
            weights = jnp.exp2(parts[c] * (scale * log2e) - best * log2e)
            for t in range(chunk // 128):
                sums = sums + weights[:, 128 * t : 128 * t + 128]
            acc = acc + jnp.dot(
                weights.astype(bf16),
                values_ref[s, c * chunk : (c + 1) * chunk, :],
                preferred_element_type=f32,
            )
        total = jnp.broadcast_to(jnp.sum(sums, axis=1, keepdims=True), (16, dim))
        best = jnp.broadcast_to(best, (16, dim))
        _, _, i = place_of(ids[s])
        stat = jnp.where(lane8 == 127, ids[s].astype(f32), jnp.zeros((8, dim), f32))
        for k in range(4):
            found_ref[s, 8 * k : 8 * k + 8, :] = tile_of(acc, k, i)
            stat = jnp.where(lane8 == 4 * k, tile_of(best, k, i), stat)
            stat = jnp.where(lane8 == 4 * k + 1, tile_of(total, k, i), stat)
        found_ref[s, 32:40, :] = stat

    ready = scores_of(0)
    for s in range(slots):
        following = scores_of(s + 1) if s + 1 < slots else None
        finish(s, *ready)
        ready = following


def merge_kernel(part_ref, mine_ref, other_ref, out_ref):
    del part_ref
    slots = mine_ref.shape[0]
    sub8 = lax.broadcasted_iota(jnp.int32, (8, 128), 0)
    my_core = lax.axis_index("core")
    places = []
    for ref in (mine_ref, other_ref):
        numbers = [ref[s, 32:40, :][0, 127].astype(jnp.int32) for s in range(slots)]
        places.append([place_of(number) for number in numbers])
    for ref, where in zip((mine_ref, other_ref), places):
        results = [
            merged(out_ref, piece, ref[s], sub8 // 4 == i) for s, (piece, _, i) in enumerate(where)
        ]
        for (piece, core, _), tiles in zip(where, results):

            @pl.when(core == my_core)
            def _():
                for k, tile in enumerate(tiles):
                    out_ref[piece, 8 * k : 8 * k + 8, :] = tile.astype(bf16)


def combine_kernel(got_ref, out_ref):
    count = got_ref.shape[0] // 2
    sub8 = lax.broadcasted_iota(jnp.int32, (8, 128), 0)
    for half in range(2):
        at = slice(half * count, (half + 1) * count)
        stat = got_ref[at, 32:40, :].astype(f32)
        factor = jnp.exp(stat - jnp.max(stat, axis=0, keepdims=True))
        total = pltpu.roll(stat, 127, 2) + pltpu.roll(stat, 126, 2)
        inverse = 1.0 / jnp.sum(factor * total, axis=0)
        rows = []
        for k in range(4):
            acc = got_ref[at, 8 * k : 8 * k + 8, :].astype(f32)
            acc = jnp.sum(acc * factor[:, :, 4 * k : 4 * k + 1], axis=0)
            rows.append(acc * inverse[:, 4 * k : 4 * k + 1])
        for k in (0, 2):
            base = 16 * half + 4 * k
            turned = pltpu.roll(rows[k + 1], 4, 0)
            out_ref[0, base : base + 8, :] = jnp.where(sub8 < 4, rows[k], turned).astype(bf16)
            turned = pltpu.roll(rows[k], 4, 0)
            out_ref[1, base : base + 8, :] = jnp.where(sub8 < 4, turned, rows[k + 1]).astype(bf16)


def shards(
    queries, prefix_keys, prefix_values, suffix_keys, suffix_values, suffix_lengths, slot_sequence
):
    kv_count = lax.axis_size("kv")
    m_count = lax.axis_size("m")
    per_device, head_count, dim = queries.shape
    local_heads = head_count // kv_count
    kv_local = prefix_keys.shape[1]
    pieces = kv_count * m_count
    slots, suffix_len = suffix_keys.shape[:2]
    swap = [(0, 1), (1, 0)]

    def across(x):
        return lax.ppermute(x, "core", swap)

    def exchange(x):
        return lax.all_to_all(x, ("kv", "m"), split_axis=0, concat_axis=0, tiled=True)

    sent = pl.pallas_call(
        ask_kernel,
        in_specs=[vmem],
        out_specs=vmem,
        out_shape=jax.ShapeDtypeStruct((kv_count, m_count, per_device * local_heads, dim), bf16),
        cost_estimate=pl.CostEstimate(flops=10**11, transcendentals=0, bytes_accessed=2**28),
        compiler_params=limit(4),
        name="ask",
    )(queries)
    mine = exchange(sent.reshape(pieces, per_device * local_heads, dim))
    other = across(mine)
    there = across(prefix_keys), across(prefix_values)

    keys = suffix_keys.reshape(slots, suffix_len * kv_local, dim)
    values = suffix_values.reshape(slots, suffix_len * kv_local, dim)
    found = pl.pallas_call(
        suffix_kernel,
        in_specs=[vmem] * 6,
        out_specs=vmem,
        out_shape=jax.ShapeDtypeStruct((slots, per_device * local_heads + 8, dim), f32),
        cost_estimate=pl.CostEstimate(flops=10**9, transcendentals=0, bytes_accessed=2**21),
        compiler_params=limit(4),
        name="suffix",
    )(*(x.reshape(1, slots) for x in (slot_sequence, suffix_lengths)), mine, other, keys, values)
    found_there = across(found)

    part = pl.pallas_call(
        prefix_kernel,
        in_specs=[vmem] * 5,
        out_specs=vmem,
        out_shape=jax.ShapeDtypeStruct((pieces, per_device * local_heads + 8, dim), bf16),
        scratch_shapes=[pltpu.VMEM((2, 2, prefix_keys.shape[0] * kv_local, dim), f32)],
        cost_estimate=pl.CostEstimate(flops=10**9, transcendentals=0, bytes_accessed=2**21),
        compiler_params=limit(6),
        name="prefix",
    )(mine, prefix_keys, prefix_values, *there)
    part = pl.pallas_call(
        merge_kernel,
        in_specs=[vmem] * 3,
        out_specs=vmem,
        out_shape=jax.ShapeDtypeStruct(part.shape, bf16),
        input_output_aliases={0: 0},
        compiler_params=limit(4),
        name="merge",
    )(part, found, found_there)

    got = exchange(part)
    return pl.pallas_call(
        combine_kernel,
        in_specs=[vmem],
        out_specs=vmem,
        out_shape=jax.ShapeDtypeStruct(queries.shape, bf16),
        compiler_params=limit(4),
        name="combine",
    )(got)


def solution(mesh):
    kv, batch = (mesh.shape[a] for a in ("kv", "batch"))
    fine = Mesh(mesh.devices.reshape(kv, batch // 2, 2), ("kv", "m", "core"))
    rows, positions = ("kv", "m", "core"), ("m", "core")
    return jax.shard_map(
        shards,
        mesh=fine,
        in_specs=(
            P(rows, None, None),
            P(positions, "kv", None),
            P(positions, "kv", None),
            P(positions, None, "kv", None),
            P(positions, None, "kv", None),
            P(positions),
            P(positions),
        ),
        out_specs=P(rows, None, None),
        check_vma=False,
    )
```

time: 55.8 us -> 54.5 us (0.977)
  waiting for transfers between devices: 2.32 us -> 1.03 us
    ppermute x4, waiting for transfers between devices: 2.32 us -> 1.03 us  [across(): return lax.ppermute(x, 'core', swap)]
  transfers between devices with their start and end apart: 4 -> 4, of which waited for: 3 -> 1; matrix products, arithmetic and copies ran while one was open for 0% -> 0% of each run, Pallas kernels for 2% -> 9%
where the time goes in v3:
time: 54.5 us; the launch traced here: 53.8 us
  blocking collectives  42.4 us (78%)
  Pallas kernels  6.52 us (12%)
  starting transfers between devices  2.95 us (5%)
  waiting for transfers between devices  1.03 us (2%)
  local copies, waits for them, and re-layouts  0.88 us (2%)
    all_to_all x2, blocking collectives, exchange(): lax.all_to_all(x, ('kv', 'm'), split_axis=0, concat_axis=0, tiled=True)  42.4 us
    pallas_call x1, Pallas kernels, shards(): pl.pallas_call(suffix_kernel, in_specs=[vmem] * 6, out_specs=vmem, out_sh...  3.68 us
    ppermute x4, starting transfers between devices, across(): return lax.ppermute(x, 'core', swap)  2.95 us
    pallas_call x1, Pallas kernels, shards(): pl.pallas_call(combine_kernel, in_specs=[vmem], out_specs=vmem, out_shape...  1.11 us
    pallas_call x1, Pallas kernels, shards(): pl.pallas_call(prefix_kernel, in_specs=[vmem] * 5, out_specs=vmem, out_sh...  1.1 us
  transfers between devices with their start and end apart: 4, of which 1 were waited for; matrix products, arithmetic and copies ran while one was open for 0% of the time, Pallas kernels for 9%

profile of v3, /device:TPU:1, one launch (start us, length us, event | category | flops | bytes accessed | tf_op | source)
XLA Modules:
  0.0 53.8 jit_solution(7828833419016229212)
XLA Ops:
  0.0 0.0 copy-start.4
  0.0 0.0 copy-start.5
  0.0 0.0 copy-start.2
  0.0 0.0 copy-start.3
  0.0 0.0 copy-start
  0.0 0.0 copy-start.6
  0.0 0.9 %copy-done.6 = bf16[2,32,128]{2,1,0:T(8,128)(2,1)S(1)} copy-done((bf16[2,32,128]{2,1,0:T(8,128)(2,1)S(1)}, bf16[2,32,128]{2,1,0:T(8,128)(2,1)}, u32[]{:S(2)}) %copy-start.6) | copy-done | bytes 16408
  0.9 0.0 copy-start.1
  0.9 24.3 %all_to_all.10.q_ref.mine_ref = bf16[64,32,128]{2,1,0:T(8,128)(2,1)S(1)} all-to-all(bf16[64,32,128]{2,1,0:T(8,128)(2,1)S(1)} %bitcast.7), channel_id=1, replica_groups=mesh['kv'=2,'m'=32,'core'=2] {'kv','m'}, dimensions={0} | all-to-all | bytes 1048576 | tf_op jit(solution)/shard_map/all_to_all | solution.py:231
  25.2 2.0 %collective-permute-start.2 = (bf16[64,32,128]{2,1,0:T(8,128)(2,1)S(1)}, bf16[64,32,128]{2,1,0:T(8,128)(2,1)S(1)}, u32[]{:S(2)}, u32[]{:S(2)}) collective-permute-start(bf16[64,32,128]{2,1,0:T(8,128)(2,1)S(1)} %all_to_all.10.q_ref.mine_ref), channel_id=1, source_target_pairs={{0,1},{1,0},{2,3},{3,2},{4,5},{5,4},{6,7},{7,6},{8,9},{9,8},{10,11... | collective-permute-start | bytes 1572872 | tf_op jit(solution)/shard_map/ppermute | solution.py:228
  27.2 0.0 copy-done.4
  27.2 0.0 collective-permute-start
  27.2 0.0 copy-done.5
  27.2 0.5 collective-permute-start.1
  27.7 1.0 %collective-permute-done.2.other_ref = bf16[64,32,128]{2,1,0:T(8,128)(2,1)S(1)} collective-permute-done((bf16[64,32,128]{2,1,0:T(8,128)(2,1)S(1)}, bf16[64,32,128]{2,1,0:T(8,128)(2,1)S(1)}, u32[]{:S(2)}, u32[]{:S(2)}) %collective-permute-start.2) | collective-permute-done | bytes 524320 | tf_op jit(solution)/shard_map/ppermute | solution.py:228
  28.7 0.0 copy-done.2
  28.7 0.0 copy-done.3
  28.7 0.0 copy-done
  28.7 0.0 copy-done.1
  28.7 3.7 %suffix.1.mine_ref = f32[4,40,128]{2,1,0:T(8,128)S(1)} custom-call(s32[1,4]{1,0:T(1,128)S(1)} %bitcast.8, s32[1,4]{1,0:T(1,128)S(1)} %bitcast.9, bf16[64,32,128]{2,1,0:T(8,128)(2,1)S(1)} %all_to_all.10.q_ref.mine_ref, bf16[64,32,128]{2,1,0:T(8,128)(2,1)S(1)} %collective-permute-done.2.other_ref, bf16[4,8192,128]{2,1,0:T(8,128)(2,1)S(1)} %bitcast.5, ...), custom_call_target="tpu_custom_call" | custom-call | flops 1000000000 | bytes 2097152 | tf_op jit(solution)/shard_map/suffix/pallas_call | solution.py:248
  32.4 0.5 collective-permute-start.3
  32.9 0.0 collective-permute-done.k1_ref
  32.9 0.0 collective-permute-done.1.v1_ref
  32.9 1.1 %prefix.1.part_ref = bf16[64,40,128]{2,1,0:T(8,128)(2,1)S(1)} custom-call(bf16[64,32,128]{2,1,0:T(8,128)(2,1)S(1)} %all_to_all.10.q_ref.mine_ref, bf16[128,4,128]{2,1,0:T(4,128)(2,1)S(1)} %copy-done.4, bf16[128,4,128]{2,1,0:T(4,128)(2,1)S(1)} %copy-done.5, bf16[128,4,128]{2,1,0:T(4,128)(2,1)S(1)} %collective-permute-done.k1_ref, ...), custom_call_target="tpu_custom_call" | custom-call | flops 1000000000 | bytes 2097152 | tf_op jit(solution)/shard_map/prefix/pallas_call | solution.py:259
  34.0 0.0 collective-permute-done.3.other_ref
  34.0 0.6 %merge.1 = bf16[64,40,128]{2,1,0:T(8,128)(2,1)S(1)} custom-call(bf16[64,40,128]{2,1,0:T(8,128)(2,1)S(1)} %prefix.1.part_ref, f32[4,40,128]{2,1,0:T(8,128)S(1)} %suffix.1.mine_ref, f32[4,40,128]{2,1,0:T(8,128)S(1)} %collective-permute-done.3.other_ref), custom_call_target="tpu_custom_call", output_to_operand_aliasing={{}: (0, {})} | custom-call | tf_op jit(solution)/shard_map/merge/pallas_call | solution.py:269
  34.6 18.1 %all_to_all.11.got_ref = bf16[64,40,128]{2,1,0:T(8,128)(2,1)S(1)} all-to-all(bf16[64,40,128]{2,1,0:T(8,128)(2,1)S(1)} %merge.1), channel_id=1, replica_groups=mesh['kv'=2,'m'=32,'core'=2] {'kv','m'}, dimensions={0} | all-to-all | bytes 1310720 | tf_op jit(solution)/shard_map/all_to_all | solution.py:231
  52.7 1.1 %combine.1 = bf16[2,32,128]{2,1,0:T(8,128)(2,1)} custom-call(bf16[64,40,128]{2,1,0:T(8,128)(2,1)S(1)} %all_to_all.11.got_ref), custom_call_target="tpu_custom_call" | custom-call | tf_op jit(solution)/shard_map/combine/pallas_call | solution.py:280
  (1 shorter events, 0.0 us)
Async XLA Ops:
  0.0 27.2 %copy-start.4 = (bf16[128,4,128]{2,1,0:T(4,128)(2,1)S(1)}, bf16[128,4,128]{2,1,0:T(4,128)(2,1)}, u32[]{:S(2)}) copy-start(bf16[128,4,128]{2,1,0:T(4,128)(2,1)} %k0_ref.1) | copy-start | bytes 393220
  0.0 27.2 %copy-start.5 = (bf16[128,4,128]{2,1,0:T(4,128)(2,1)S(1)}, bf16[128,4,128]{2,1,0:T(4,128)(2,1)}, u32[]{:S(2)}) copy-start(bf16[128,4,128]{2,1,0:T(4,128)(2,1)} %v0_ref.1) | copy-start | bytes 393220
  0.0 28.7 %copy-start.2 = (s32[4]{0:T(128)S(1)}, s32[4]{0:T(128)}, u32[]{:S(2)}) copy-start(s32[4]{0:T(128)} %param.13) | copy-start | bytes 52
  0.0 28.7 %copy-start.3 = (s32[4]{0:T(128)S(1)}, s32[4]{0:T(128)}, u32[]{:S(2)}) copy-start(s32[4]{0:T(128)} %param.12) | copy-start | bytes 52
  0.0 28.7 %copy-start = (bf16[4,2048,4,128]{3,2,1,0:T(4,128)(2,1)S(1)}, bf16[4,2048,4,128]{3,2,1,0:T(4,128)(2,1)}, u32[]{:S(2)}) copy-start(bf16[4,2048,4,128]{3,2,1,0:T(4,128)(2,1)} %param.10) | copy-start | bytes 25165828
  0.0 0.9 %copy-start.6 = (bf16[2,32,128]{2,1,0:T(8,128)(2,1)S(1)}, bf16[2,32,128]{2,1,0:T(8,128)(2,1)}, u32[]{:S(2)}) copy-start(bf16[2,32,128]{2,1,0:T(8,128)(2,1)} %queries_ref.1) | copy-start | bytes 49156
  0.9 27.8 %copy-start.1 = (bf16[4,2048,4,128]{3,2,1,0:T(4,128)(2,1)S(1)}, bf16[4,2048,4,128]{3,2,1,0:T(4,128)(2,1)}, u32[]{:S(2)}) copy-start(bf16[4,2048,4,128]{3,2,1,0:T(4,128)(2,1)} %param.11) | copy-start | bytes 25165828
  25.2 3.5 %collective-permute-start.2 = (bf16[64,32,128]{2,1,0:T(8,128)(2,1)S(1)}, bf16[64,32,128]{2,1,0:T(8,128)(2,1)S(1)}, u32[]{:S(2)}, u32[]{:S(2)}) collective-permute-start(bf16[64,32,128]{2,1,0:T(8,128)(2,1)S(1)} %all_to_all.10.q_ref.mine_ref), channel_id=1, source_target_pairs={{0,1},{1,0},{2,3},{3,2},{4,5},{5,4},{6,7},{7,6},{8,9},{9,8},{10,11... | collective-permute-start | bytes 1572872 | tf_op jit(solution)/shard_map/ppermute | solution.py:228
  27.2 5.7 %collective-permute-start = (bf16[128,4,128]{2,1,0:T(4,128)(2,1)S(1)}, bf16[128,4,128]{2,1,0:T(4,128)(2,1)S(1)}, u32[]{:S(2)}, u32[]{:S(2)}) collective-permute-start(bf16[128,4,128]{2,1,0:T(4,128)(2,1)S(1)} %copy-done.4), channel_id=1, source_target_pairs={{0,1},{1,0},{2,3},{3,2},{4,5},{5,4},{6,7},{7,6},{8,9},{9,8},{10,11... | collective-permute-start | bytes 393224 | tf_op jit(solution)/shard_map/ppermute | solution.py:228
  27.2 5.7 %collective-permute-start.1 = (bf16[128,4,128]{2,1,0:T(4,128)(2,1)S(1)}, bf16[128,4,128]{2,1,0:T(4,128)(2,1)S(1)}, u32[]{:S(2)}, u32[]{:S(2)}) collective-permute-start(bf16[128,4,128]{2,1,0:T(4,128)(2,1)S(1)} %copy-done.5), channel_id=1, source_target_pairs={{0,1},{1,0},{2,3},{3,2},{4,5},{5,4},{6,7},{7,6},{8,9},{9,8},{10,11... | collective-permute-start | bytes 393224 | tf_op jit(solution)/shard_map/ppermute | solution.py:228
  32.4 1.6 %collective-permute-start.3 = (f32[4,40,128]{2,1,0:T(8,128)S(1)}, f32[4,40,128]{2,1,0:T(8,128)S(1)}, u32[]{:S(2)}, u32[]{:S(2)}) collective-permute-start(f32[4,40,128]{2,1,0:T(8,128)S(1)} %suffix.1.mine_ref), channel_id=1, source_target_pairs={{0,1},{1,0},{2,3},{3,2},{4,5},{5,4},{6,7},{7,6},{8,9},{9,8},{10,11... | collective-permute-start | bytes 245768 | tf_op jit(solution)/shard_map/ppermute | solution.py:228

commit v4 on v3

--- a/solution.py
+++ b/solution.py
@@ -29,7 +29,12 @@
     return [row[0, n] for n in range(row.shape[1])]
 
 
-def ask_kernel(queries_ref, out_ref):
+def first_kernel(out_ref):
+    out_ref[...] = jnp.zeros(out_ref.shape, out_ref.dtype)
+
+
+def ask_kernel(queries_ref, first_ref, out_ref):
+    del first_ref
     groups, copies = out_ref.shape[:2]
     sub8 = lax.broadcasted_iota(jnp.int32, (8, out_ref.shape[3]), 0)
     for g in range(groups):
@@ -106,6 +111,16 @@
     return [*tiles, jnp.where(used, stat, old_stat)]
 
 
+def reached_kernel(mine_ref, out_ref):
+    out_ref[...] = mine_ref[0, :8, :]
+
+
+def pick_kernel(ids_ref, mine_ref, reached_ref, out_ref):
+    del reached_ref
+    for s, sequence in enumerate(scalars_of(ids_ref)):
+        out_ref[s] = mine_ref[place_of(sequence)[0]]
+
+
 def suffix_kernel(ids_ref, len_ref, mine_ref, other_ref, keys_ref, values_ref, found_ref):
     slots, wide, dim = keys_ref.shape
     scale = dim ** (-0.5)
@@ -122,7 +137,7 @@
     def scores_of(s):
         piece, core, i = place_of(ids[s])
         length = lengths[s]
-        q = jnp.where(core == my_core, mine_ref[piece].astype(f32), other_ref[piece].astype(f32))
+        q = jnp.where(core == my_core, mine_ref[piece].astype(f32), other_ref[s].astype(f32))
         pairs = []
         for k in (0, 2):
             even, odd = q[8 * k : 8 * k + 8], q[8 * k + 8 : 8 * k + 16]
@@ -230,17 +245,42 @@
     def exchange(x):
         return lax.all_to_all(x, ("kv", "m"), split_axis=0, concat_axis=0, tiled=True)
 
+    first = pl.pallas_call(
+        first_kernel,
+        out_specs=vmem,
+        out_shape=jax.ShapeDtypeStruct((8, 128), f32),
+        cost_estimate=pl.CostEstimate(flops=10**11, transcendentals=0, bytes_accessed=2**28),
+        compiler_params=limit(1),
+        name="first",
+    )()
     sent = pl.pallas_call(
         ask_kernel,
-        in_specs=[vmem],
+        in_specs=[vmem] * 2,
         out_specs=vmem,
         out_shape=jax.ShapeDtypeStruct((kv_count, m_count, per_device * local_heads, dim), bf16),
-        cost_estimate=pl.CostEstimate(flops=10**11, transcendentals=0, bytes_accessed=2**28),
         compiler_params=limit(4),
         name="ask",
-    )(queries)
+    )(queries, first)
+    told, _ = lax.optimization_barrier((slot_sequence, first))
+    ids_there = across(told)
     mine = exchange(sent.reshape(pieces, per_device * local_heads, dim))
-    other = across(mine)
+    reached = pl.pallas_call(
+        reached_kernel,
+        in_specs=[vmem],
+        out_specs=vmem,
+        out_shape=jax.ShapeDtypeStruct((8, dim), bf16),
+        compiler_params=limit(1),
+        name="reached",
+    )(mine)
+    picked = pl.pallas_call(
+        pick_kernel,
+        in_specs=[vmem] * 3,
+        out_specs=vmem,
+        out_shape=jax.ShapeDtypeStruct((slots, per_device * local_heads, dim), bf16),
+        compiler_params=limit(1),
+        name="pick",
+    )(ids_there.reshape(1, slots), mine, reached)
+    other = across(picked)
     there = across(prefix_keys), across(prefix_values)
 
     keys = suffix_keys.reshape(slots, suffix_len * kv_local, dim)

time: 54.5 us -> 61.4 us (1.13)
  blocking collectives: 42.4 us -> 18.1 us
  starting transfers between devices: 2.95 us -> 16 us
  waiting for transfers between devices: 1.03 us -> 11.6 us
  local copies, waits for them, and re-layouts: 0.88 us -> 7.46 us
  Pallas kernels: 6.52 us -> 7.46 us
    all_to_all x2 -> x1, blocking collectives: 42.4 us -> 18.1 us  [exchange(): lax.all_to_all(x, ('kv', 'm'), split_axis=0, concat_axis=0, tiled=True)]
    all_to_all x0 -> x1, starting transfers between devices: none -> 12 us  [exchange(): lax.all_to_all(x, ('kv', 'm'), split_axis=0, concat_axis=0, tiled=True)]
    all_to_all x0 -> x1, waiting for transfers between devices: none -> 10.7 us  [exchange(): lax.all_to_all(x, ('kv', 'm'), split_axis=0, concat_axis=0, tiled=True)]
    unnamed x14, local copies, waits for them, and re-layouts: 0.88 us -> 7.46 us
    ppermute x4 -> x5, starting transfers between devices: 2.95 us -> 4.04 us  [across(): return lax.ppermute(x, 'core', swap)]
    pallas_call x1 -> x4, Pallas kernels: 0.04 us -> 0.97 us  [the longest x1 0.83 us: shards(): pl.pallas_call(ask_kernel, in_specs=[vmem] * 2, out_specs=vmem, out_shape...]
  transfers between devices with their start and end apart: 4 -> 6, of which waited for: 1 -> 2; matrix products, arithmetic and copies ran while one was open for 0% -> 0% of each run, Pallas kernels for 9% -> 8%
where the time goes in v4:
time: 61.4 us; the launch traced here: 60.7 us
  blocking collectives  18.1 us (29%)
  starting transfers between devices  16 us (26%)
  waiting for transfers between devices  11.6 us (19%)
  local copies, waits for them, and re-layouts  7.46 us (12%)
  Pallas kernels  7.46 us (12%)
    all_to_all x1, blocking collectives, exchange(): lax.all_to_all(x, ('kv', 'm'), split_axis=0, concat_axis=0, tiled=True)  18.1 us
    all_to_all x1, starting transfers between devices, exchange(): lax.all_to_all(x, ('kv', 'm'), split_axis=0, concat_axis=0, tiled=True)  12 us
    all_to_all x1, waiting for transfers between devices, exchange(): lax.all_to_all(x, ('kv', 'm'), split_axis=0, concat_axis=0, tiled=True)  10.7 us
    unnamed x14, local copies, waits for them, and re-layouts  7.46 us
    ppermute x5, starting transfers between devices, across(): return lax.ppermute(x, 'core', swap)  4.04 us
    pallas_call x1, Pallas kernels, shards(): pl.pallas_call(suffix_kernel, in_specs=[vmem] * 6, out_specs=vmem, out_sh...  3.68 us
  transfers between devices with their start and end apart: 6, of which 2 were waited for; matrix products, arithmetic and copies ran while one was open for 0% of the time, Pallas kernels for 8%

profile of v4, /device:TPU:1, one launch (start us, length us, event | category | flops | bytes accessed | tf_op | source)
XLA Modules:
  0.0 60.7 jit_solution(10418316940598111796)
XLA Ops:
  0.0 0.0 copy-start.2
  0.0 0.0 copy-start.5
  0.0 0.0 copy-start.6
  0.0 0.0 copy-start.3
  0.0 0.0 copy-start.4
  0.0 0.7 %copy-done.2 = bf16[2,32,128]{2,1,0:T(8,128)(2,1)S(1)} copy-done((bf16[2,32,128]{2,1,0:T(8,128)(2,1)S(1)}, bf16[2,32,128]{2,1,0:T(8,128)(2,1)}, u32[]{:S(2)}) %copy-start.2) | copy-done | bytes 16408
  0.7 0.8 %ask.1 = bf16[2,32,32,128]{3,2,1,0:T(8,128)(2,1)} custom-call(bf16[2,32,128]{2,1,0:T(8,128)(2,1)S(1)} %copy-done.2, f32[8,128]{1,0:T(8,128)S(1)} %first.1.first_ref), custom_call_target="tpu_custom_call" | custom-call | tf_op jit(solution)/shard_map/ask/pallas_call | solution.py:256
  1.6 12.0 %all-to-all-start = ((bf16[64,32,128]{2,1,0:T(8,128)(2,1)}), bf16[64,32,128]{2,1,0:T(8,128)(2,1)S(1)}, u32[]{:S(2)}, u32[]{:S(2)}) async-start(bf16[64,32,128]{2,1,0:T(8,128)(2,1)} %bitcast), calls=%async_computation | async-start | bytes 1048576 | tf_op jit(solution)/shard_map/all_to_all | solution.py:246
  13.5 0.0 copy-done.5
  13.5 1.0 %collective-permute-start = (bf16[128,4,128]{2,1,0:T(4,128)(2,1)S(1)}, bf16[128,4,128]{2,1,0:T(4,128)(2,1)S(1)}, u32[]{:S(2)}, u32[]{:S(2)}) collective-permute-start(bf16[128,4,128]{2,1,0:T(4,128)(2,1)S(1)} %copy-done.5), channel_id=1, source_target_pairs={{0,1},{1,0},{2,3},{3,2},{4,5},{5,4},{6,7},{7,6},{8,9},{9,8},{10,11... | collective-permute-start | bytes 393224 | tf_op jit(solution)/shard_map/ppermute | solution.py:243
  14.6 0.0 copy-done.6
  14.6 0.1 collective-permute-start.1
  14.7 0.0 copy-done.3
  14.7 0.4 collective-permute-start.2
  15.1 10.7 %all-to-all-done.q_ref.mine_ref = bf16[64,32,128]{2,1,0:T(8,128)(2,1)S(1)} async-done(((bf16[64,32,128]{2,1,0:T(8,128)(2,1)}), bf16[64,32,128]{2,1,0:T(8,128)(2,1)S(1)}, u32[]{:S(2)}, u32[]{:S(2)}) %all-to-all-start) | async-done | bytes 524320 | tf_op jit(solution)/shard_map/all_to_all | solution.py:246
  25.8 0.0 collective-permute-done.2
  25.8 0.1 pick.1
  25.9 2.1 %collective-permute-start.3 = (bf16[4,32,128]{2,1,0:T(8,128)(2,1)S(1)}, bf16[4,32,128]{2,1,0:T(8,128)(2,1)S(1)}, u32[]{:S(2)}, u32[]{:S(2)}) collective-permute-start(bf16[4,32,128]{2,1,0:T(8,128)(2,1)S(1)} %pick.1), channel_id=1, source_target_pairs={{0,1},{1,0},{2,3},{3,2},{4,5},{5,4},{6,7},{7,6},{8,9},{9,8},{10,11... | collective-permute-start | bytes 98312 | tf_op jit(solution)/shard_map/ppermute | solution.py:243
  28.0 0.9 %collective-permute-done.3.other_ref = bf16[4,32,128]{2,1,0:T(8,128)(2,1)S(1)} collective-permute-done((bf16[4,32,128]{2,1,0:T(8,128)(2,1)S(1)}, bf16[4,32,128]{2,1,0:T(8,128)(2,1)S(1)}, u32[]{:S(2)}, u32[]{:S(2)}) %collective-permute-start.3) | collective-permute-done | bytes 32800 | tf_op jit(solution)/shard_map/ppermute | solution.py:243
  28.8 0.0 copy-done.4
  28.8 0.0 copy-start
  28.8 3.4 %copy-done = bf16[4,2048,4,128]{3,2,1,0:T(4,128)(2,1)S(1)} copy-done((bf16[4,2048,4,128]{3,2,1,0:T(4,128)(2,1)S(1)}, bf16[4,2048,4,128]{3,2,1,0:T(4,128)(2,1)}, u32[]{:S(2)}) %copy-start) | copy-done | bytes 8388632
  32.2 3.4 %copy-done.1 = bf16[4,2048,4,128]{3,2,1,0:T(4,128)(2,1)S(1)} copy-done((bf16[4,2048,4,128]{3,2,1,0:T(4,128)(2,1)S(1)}, bf16[4,2048,4,128]{3,2,1,0:T(4,128)(2,1)}, u32[]{:S(2)}) %copy-start.1) | copy-done | bytes 8388632
  35.6 3.7 %suffix.1.mine_ref = f32[4,40,128]{2,1,0:T(8,128)S(1)} custom-call(s32[1,4]{1,0:T(1,128)S(1)} %bitcast.8, s32[1,4]{1,0:T(1,128)S(1)} %bitcast.9, bf16[64,32,128]{2,1,0:T(8,128)(2,1)S(1)} %all-to-all-done.q_ref.mine_ref, bf16[4,32,128]{2,1,0:T(8,128)(2,1)S(1)} %collective-permute-done.3.other_ref, bf16[4,8192,128]{2,1,0:T(8,128)(2,1)S(1)} %bitcast.6, ...), custom_call_target="tpu_custom_call" | custom-call | flops 1000000000 | bytes 2097152 | tf_op jit(solution)/shard_map/suffix/pallas_call | solution.py:288
  39.3 0.4 collective-permute-start.4
  39.7 0.0 collective-permute-done.k1_ref
  39.7 0.0 collective-permute-done.1.v1_ref
  39.7 1.1 %prefix.1.part_ref = bf16[64,40,128]{2,1,0:T(8,128)(2,1)S(1)} custom-call(bf16[64,32,128]{2,1,0:T(8,128)(2,1)S(1)} %all-to-all-done.q_ref.mine_ref, bf16[128,4,128]{2,1,0:T(4,128)(2,1)S(1)} %copy-done.5, bf16[128,4,128]{2,1,0:T(4,128)(2,1)S(1)} %copy-done.6, bf16[128,4,128]{2,1,0:T(4,128)(2,1)S(1)} %collective-permute-done.k1_ref, ...), custom_call_target="tpu_custom_call" | custom-call | flops 1000000000 | bytes 2097152 | tf_op jit(solution)/shard_map/prefix/pallas_call | solution.py:299
  40.8 0.0 collective-permute-done.4.other_ref
  40.8 0.6 merge.1
  41.4 18.1 %all_to_all.10.got_ref = bf16[64,40,128]{2,1,0:T(8,128)(2,1)S(1)} all-to-all(bf16[64,40,128]{2,1,0:T(8,128)(2,1)S(1)} %merge.1), channel_id=1, replica_groups=mesh['kv'=2,'m'=32,'core'=2] {'kv','m'}, dimensions={0} | all-to-all | bytes 1310720 | tf_op jit(solution)/shard_map/all_to_all | solution.py:246
  59.6 1.1 %combine.1 = bf16[2,32,128]{2,1,0:T(8,128)(2,1)} custom-call(bf16[64,40,128]{2,1,0:T(8,128)(2,1)S(1)} %all_to_all.10.got_ref), custom_call_target="tpu_custom_call" | custom-call | tf_op jit(solution)/shard_map/combine/pallas_call | solution.py:320
  (3 shorter events, 0.0 us)
Async XLA Ops:
  0.0 0.7 %copy-start.2 = (bf16[2,32,128]{2,1,0:T(8,128)(2,1)S(1)}, bf16[2,32,128]{2,1,0:T(8,128)(2,1)}, u32[]{:S(2)}) copy-start(bf16[2,32,128]{2,1,0:T(8,128)(2,1)} %queries_ref.1) | copy-start | bytes 49156
  0.0 13.5 %copy-start.5 = (bf16[128,4,128]{2,1,0:T(4,128)(2,1)S(1)}, bf16[128,4,128]{2,1,0:T(4,128)(2,1)}, u32[]{:S(2)}) copy-start(bf16[128,4,128]{2,1,0:T(4,128)(2,1)} %k0_ref.1) | copy-start | bytes 393220
  0.0 14.6 %copy-start.6 = (bf16[128,4,128]{2,1,0:T(4,128)(2,1)S(1)}, bf16[128,4,128]{2,1,0:T(4,128)(2,1)}, u32[]{:S(2)}) copy-start(bf16[128,4,128]{2,1,0:T(4,128)(2,1)} %v0_ref.1) | copy-start | bytes 393220
  0.0 14.7 %copy-start.3 = (s32[4]{0:T(128)S(1)}, s32[4]{0:T(128)}, u32[]{:S(2)}) copy-start(s32[4]{0:T(128)} %param.13) | copy-start | bytes 52
  0.0 28.8 %copy-start.4 = (s32[4]{0:T(128)S(1)}, s32[4]{0:T(128)}, u32[]{:S(2)}) copy-start(s32[4]{0:T(128)} %param.12) | copy-start | bytes 52
  1.6 24.2 %all-to-all-start = ((bf16[64,32,128]{2,1,0:T(8,128)(2,1)}), bf16[64,32,128]{2,1,0:T(8,128)(2,1)S(1)}, u32[]{:S(2)}, u32[]{:S(2)}) async-start(bf16[64,32,128]{2,1,0:T(8,128)(2,1)} %bitcast), calls=%async_computation | async-start | bytes 1048576 | tf_op jit(solution)/shard_map/all_to_all | solution.py:246
  13.5 26.2 %collective-permute-start = (bf16[128,4,128]{2,1,0:T(4,128)(2,1)S(1)}, bf16[128,4,128]{2,1,0:T(4,128)(2,1)S(1)}, u32[]{:S(2)}, u32[]{:S(2)}) collective-permute-start(bf16[128,4,128]{2,1,0:T(4,128)(2,1)S(1)} %copy-done.5), channel_id=1, source_target_pairs={{0,1},{1,0},{2,3},{3,2},{4,5},{5,4},{6,7},{7,6},{8,9},{9,8},{10,11... | collective-permute-start | bytes 393224 | tf_op jit(solution)/shard_map/ppermute | solution.py:243
  14.6 25.2 %collective-permute-start.1 = (bf16[128,4,128]{2,1,0:T(4,128)(2,1)S(1)}, bf16[128,4,128]{2,1,0:T(4,128)(2,1)S(1)}, u32[]{:S(2)}, u32[]{:S(2)}) collective-permute-start(bf16[128,4,128]{2,1,0:T(4,128)(2,1)S(1)} %copy-done.6), channel_id=1, source_target_pairs={{0,1},{1,0},{2,3},{3,2},{4,5},{5,4},{6,7},{7,6},{8,9},{9,8},{10,11... | collective-permute-start | bytes 393224 | tf_op jit(solution)/shard_map/ppermute | solution.py:243
  14.7 11.1 %collective-permute-start.2 = (s32[4]{0:T(128)S(1)}, s32[4]{0:T(128)S(1)}, u32[]{:S(2)}, u32[]{:S(2)}) collective-permute-start(s32[4]{0:T(128)S(1)} %copy-done.3), channel_id=1, source_target_pairs={{0,1},{1,0},{2,3},{3,2},{4,5},{5,4},{6,7},{7,6},{8,9},{9,8},{10,11... | collective-permute-start | bytes 56 | tf_op jit(solution)/shard_map/ppermute | solution.py:243
  25.9 2.9 %collective-permute-start.3 = (bf16[4,32,128]{2,1,0:T(8,128)(2,1)S(1)}, bf16[4,32,128]{2,1,0:T(8,128)(2,1)S(1)}, u32[]{:S(2)}, u32[]{:S(2)}) collective-permute-start(bf16[4,32,128]{2,1,0:T(8,128)(2,1)S(1)} %pick.1), channel_id=1, source_target_pairs={{0,1},{1,0},{2,3},{3,2},{4,5},{5,4},{6,7},{7,6},{8,9},{9,8},{10,11... | collective-permute-start | bytes 98312 | tf_op jit(solution)/shard_map/ppermute | solution.py:243
  28.8 3.4 %copy-start = (bf16[4,2048,4,128]{3,2,1,0:T(4,128)(2,1)S(1)}, bf16[4,2048,4,128]{3,2,1,0:T(4,128)(2,1)}, u32[]{:S(2)}) copy-start(bf16[4,2048,4,128]{3,2,1,0:T(4,128)(2,1)} %param.10) | copy-start | bytes 25165828
  32.2 3.4 %copy-start.1 = (bf16[4,2048,4,128]{3,2,1,0:T(4,128)(2,1)S(1)}, bf16[4,2048,4,128]{3,2,1,0:T(4,128)(2,1)}, u32[]{:S(2)}) copy-start(bf16[4,2048,4,128]{3,2,1,0:T(4,128)(2,1)} %param.11) | copy-start | bytes 25165828
  39.3 1.5 %collective-permute-start.4 = (f32[4,40,128]{2,1,0:T(8,128)S(1)}, f32[4,40,128]{2,1,0:T(8,128)S(1)}, u32[]{:S(2)}, u32[]{:S(2)}) collective-permute-start(f32[4,40,128]{2,1,0:T(8,128)S(1)} %suffix.1.mine_ref), channel_id=1, source_target_pairs={{0,1},{1,0},{2,3},{3,2},{4,5},{5,4},{6,7},{7,6},{8,9},{9,8},{10,11... | collective-permute-start | bytes 245768 | tf_op jit(solution)/shard_map/ppermute | solution.py:243

commit v5 on v4

--- a/solution.py
+++ b/solution.py
@@ -61,6 +61,7 @@
     pieces = q_ref.shape[0]
     positions, kv_local, dim = k0_ref.shape
     scale = dim ** (-0.5)
+    log2e = 1.4426950408889634
     rows = pieces * 8
     lane = lax.broadcasted_iota(jnp.int32, (rows, 128), 1)
     stat = jnp.zeros((rows, 128), f32)
@@ -75,9 +76,9 @@
     for k in range(kv_local):
         q = q_ref[:, 8 * k : 8 * k + 8, :].astype(f32).reshape(rows, dim).astype(bf16)
         keys, values = block_of(0, k), block_of(1, k)
-        scores = nt_dot(q, keys) * scale
-        best = rounded(jnp.max(scores, axis=1, keepdims=True))
-        weights = jnp.exp(scores - best)
+        scores = nt_dot(q, keys)
+        best = rounded(jnp.max(scores, axis=1, keepdims=True) * scale)
+        weights = jnp.exp2(scores * (scale * log2e) - best * log2e)
         total = jnp.sum(weights, axis=1, keepdims=True)
         acc = jnp.dot(weights.astype(bf16), values, preferred_element_type=f32)
         out_ref[:, 8 * k : 8 * k + 8, :] = acc.reshape(pieces, 8, dim).astype(bf16)

time: 61.4 us -> 61.4 us (level)
  no operation moved by 1% of the time
where the time goes in v5:
time: 61.4 us; the launch traced here: 60.6 us
  blocking collectives  18.1 us (29%)
  starting transfers between devices  16 us (26%)
  waiting for transfers between devices  11.6 us (19%)
  local copies, waits for them, and re-layouts  7.46 us (12%)
  Pallas kernels  7.43 us (12%)
    all_to_all x1, blocking collectives, exchange(): lax.all_to_all(x, ('kv', 'm'), split_axis=0, concat_axis=0, tiled=True)  18.1 us
    all_to_all x1, starting transfers between devices, exchange(): lax.all_to_all(x, ('kv', 'm'), split_axis=0, concat_axis=0, tiled=True)  12 us
    all_to_all x1, waiting for transfers between devices, exchange(): lax.all_to_all(x, ('kv', 'm'), split_axis=0, concat_axis=0, tiled=True)  10.7 us
    unnamed x14, local copies, waits for them, and re-layouts  7.46 us
    ppermute x5, starting transfers between devices, across(): return lax.ppermute(x, 'core', swap)  4.04 us
    pallas_call x1, Pallas kernels, shards(): pl.pallas_call(suffix_kernel, in_specs=[vmem] * 6, out_specs=vmem, out_sh...  3.68 us
  transfers between devices with their start and end apart: 6, of which 2 were waited for; matrix products, arithmetic and copies ran while one was open for 0% of the time, Pallas kernels for 8%

profile of v5, /device:TPU:1, one launch (start us, length us, event | category | flops | bytes accessed | tf_op | source)
XLA Modules:
  0.0 60.6 jit_solution(9211990802104734396)
XLA Ops:
  0.0 0.0 copy-start.2
  0.0 0.0 copy-start.5
  0.0 0.0 copy-start.6
  0.0 0.0 copy-start.3
  0.0 0.0 copy-start.4
  0.0 0.7 %copy-done.2 = bf16[2,32,128]{2,1,0:T(8,128)(2,1)S(1)} copy-done((bf16[2,32,128]{2,1,0:T(8,128)(2,1)S(1)}, bf16[2,32,128]{2,1,0:T(8,128)(2,1)}, u32[]{:S(2)}) %copy-start.2) | copy-done | bytes 16408
  0.7 0.8 %ask.1 = bf16[2,32,32,128]{3,2,1,0:T(8,128)(2,1)} custom-call(bf16[2,32,128]{2,1,0:T(8,128)(2,1)S(1)} %copy-done.2, f32[8,128]{1,0:T(8,128)S(1)} %first.1.first_ref), custom_call_target="tpu_custom_call" | custom-call | tf_op jit(solution)/shard_map/ask/pallas_call | solution.py:257
  1.6 12.0 %all-to-all-start = ((bf16[64,32,128]{2,1,0:T(8,128)(2,1)}), bf16[64,32,128]{2,1,0:T(8,128)(2,1)S(1)}, u32[]{:S(2)}, u32[]{:S(2)}) async-start(bf16[64,32,128]{2,1,0:T(8,128)(2,1)} %bitcast), calls=%async_computation | async-start | bytes 1048576 | tf_op jit(solution)/shard_map/all_to_all | solution.py:247
  13.5 0.0 copy-done.5
  13.5 1.0 %collective-permute-start = (bf16[128,4,128]{2,1,0:T(4,128)(2,1)S(1)}, bf16[128,4,128]{2,1,0:T(4,128)(2,1)S(1)}, u32[]{:S(2)}, u32[]{:S(2)}) collective-permute-start(bf16[128,4,128]{2,1,0:T(4,128)(2,1)S(1)} %copy-done.5), channel_id=1, source_target_pairs={{0,1},{1,0},{2,3},{3,2},{4,5},{5,4},{6,7},{7,6},{8,9},{9,8},{10,11... | collective-permute-start | bytes 393224 | tf_op jit(solution)/shard_map/ppermute | solution.py:244
  14.6 0.0 copy-done.6
  14.6 0.1 collective-permute-start.1
  14.7 0.0 copy-done.3
  14.7 0.4 collective-permute-start.2
  15.1 10.7 %all-to-all-done.q_ref.mine_ref = bf16[64,32,128]{2,1,0:T(8,128)(2,1)S(1)} async-done(((bf16[64,32,128]{2,1,0:T(8,128)(2,1)}), bf16[64,32,128]{2,1,0:T(8,128)(2,1)S(1)}, u32[]{:S(2)}, u32[]{:S(2)}) %all-to-all-start) | async-done | bytes 524320 | tf_op jit(solution)/shard_map/all_to_all | solution.py:247
  25.8 0.0 collective-permute-done.2
  25.8 0.1 pick.1
  25.9 2.1 %collective-permute-start.3 = (bf16[4,32,128]{2,1,0:T(8,128)(2,1)S(1)}, bf16[4,32,128]{2,1,0:T(8,128)(2,1)S(1)}, u32[]{:S(2)}, u32[]{:S(2)}) collective-permute-start(bf16[4,32,128]{2,1,0:T(8,128)(2,1)S(1)} %pick.1), channel_id=1, source_target_pairs={{0,1},{1,0},{2,3},{3,2},{4,5},{5,4},{6,7},{7,6},{8,9},{9,8},{10,11... | collective-permute-start | bytes 98312 | tf_op jit(solution)/shard_map/ppermute | solution.py:244
  28.0 0.9 %collective-permute-done.3.other_ref = bf16[4,32,128]{2,1,0:T(8,128)(2,1)S(1)} collective-permute-done((bf16[4,32,128]{2,1,0:T(8,128)(2,1)S(1)}, bf16[4,32,128]{2,1,0:T(8,128)(2,1)S(1)}, u32[]{:S(2)}, u32[]{:S(2)}) %collective-permute-start.3) | collective-permute-done | bytes 32800 | tf_op jit(solution)/shard_map/ppermute | solution.py:244
  28.8 0.0 copy-done.4
  28.8 0.0 copy-start
  28.8 3.4 %copy-done = bf16[4,2048,4,128]{3,2,1,0:T(4,128)(2,1)S(1)} copy-done((bf16[4,2048,4,128]{3,2,1,0:T(4,128)(2,1)S(1)}, bf16[4,2048,4,128]{3,2,1,0:T(4,128)(2,1)}, u32[]{:S(2)}) %copy-start) | copy-done | bytes 8388632
  32.2 3.4 %copy-done.1 = bf16[4,2048,4,128]{3,2,1,0:T(4,128)(2,1)S(1)} copy-done((bf16[4,2048,4,128]{3,2,1,0:T(4,128)(2,1)S(1)}, bf16[4,2048,4,128]{3,2,1,0:T(4,128)(2,1)}, u32[]{:S(2)}) %copy-start.1) | copy-done | bytes 8388632
  35.6 3.7 %suffix.1.mine_ref = f32[4,40,128]{2,1,0:T(8,128)S(1)} custom-call(s32[1,4]{1,0:T(1,128)S(1)} %bitcast.8, s32[1,4]{1,0:T(1,128)S(1)} %bitcast.9, bf16[64,32,128]{2,1,0:T(8,128)(2,1)S(1)} %all-to-all-done.q_ref.mine_ref, bf16[4,32,128]{2,1,0:T(8,128)(2,1)S(1)} %collective-permute-done.3.other_ref, bf16[4,8192,128]{2,1,0:T(8,128)(2,1)S(1)} %bitcast.6, ...), custom_call_target="tpu_custom_call" | custom-call | flops 1000000000 | bytes 2097152 | tf_op jit(solution)/shard_map/suffix/pallas_call | solution.py:289
  39.3 0.4 collective-permute-start.4
  39.7 0.0 collective-permute-done.k1_ref
  39.7 0.0 collective-permute-done.1.v1_ref
  39.7 1.1 %prefix.1.part_ref = bf16[64,40,128]{2,1,0:T(8,128)(2,1)S(1)} custom-call(bf16[64,32,128]{2,1,0:T(8,128)(2,1)S(1)} %all-to-all-done.q_ref.mine_ref, bf16[128,4,128]{2,1,0:T(4,128)(2,1)S(1)} %copy-done.5, bf16[128,4,128]{2,1,0:T(4,128)(2,1)S(1)} %copy-done.6, bf16[128,4,128]{2,1,0:T(4,128)(2,1)S(1)} %collective-permute-done.k1_ref, ...), custom_call_target="tpu_custom_call" | custom-call | flops 1000000000 | bytes 2097152 | tf_op jit(solution)/shard_map/prefix/pallas_call | solution.py:300
  40.8 0.0 collective-permute-done.4.other_ref
  40.8 0.6 merge.1
  41.4 18.1 %all_to_all.10.got_ref = bf16[64,40,128]{2,1,0:T(8,128)(2,1)S(1)} all-to-all(bf16[64,40,128]{2,1,0:T(8,128)(2,1)S(1)} %merge.1), channel_id=1, replica_groups=mesh['kv'=2,'m'=32,'core'=2] {'kv','m'}, dimensions={0} | all-to-all | bytes 1310720 | tf_op jit(solution)/shard_map/all_to_all | solution.py:247
  59.5 1.1 %combine.1 = bf16[2,32,128]{2,1,0:T(8,128)(2,1)} custom-call(bf16[64,40,128]{2,1,0:T(8,128)(2,1)S(1)} %all_to_all.10.got_ref), custom_call_target="tpu_custom_call" | custom-call | tf_op jit(solution)/shard_map/combine/pallas_call | solution.py:321
  (3 shorter events, 0.0 us)
Async XLA Ops:
  0.0 0.7 %copy-start.2 = (bf16[2,32,128]{2,1,0:T(8,128)(2,1)S(1)}, bf16[2,32,128]{2,1,0:T(8,128)(2,1)}, u32[]{:S(2)}) copy-start(bf16[2,32,128]{2,1,0:T(8,128)(2,1)} %queries_ref.1) | copy-start | bytes 49156
  0.0 13.5 %copy-start.5 = (bf16[128,4,128]{2,1,0:T(4,128)(2,1)S(1)}, bf16[128,4,128]{2,1,0:T(4,128)(2,1)}, u32[]{:S(2)}) copy-start(bf16[128,4,128]{2,1,0:T(4,128)(2,1)} %k0_ref.1) | copy-start | bytes 393220
  0.0 14.6 %copy-start.6 = (bf16[128,4,128]{2,1,0:T(4,128)(2,1)S(1)}, bf16[128,4,128]{2,1,0:T(4,128)(2,1)}, u32[]{:S(2)}) copy-start(bf16[128,4,128]{2,1,0:T(4,128)(2,1)} %v0_ref.1) | copy-start | bytes 393220
  0.0 14.7 %copy-start.3 = (s32[4]{0:T(128)S(1)}, s32[4]{0:T(128)}, u32[]{:S(2)}) copy-start(s32[4]{0:T(128)} %param.13) | copy-start | bytes 52
  0.0 28.8 %copy-start.4 = (s32[4]{0:T(128)S(1)}, s32[4]{0:T(128)}, u32[]{:S(2)}) copy-start(s32[4]{0:T(128)} %param.12) | copy-start | bytes 52
  1.6 24.2 %all-to-all-start = ((bf16[64,32,128]{2,1,0:T(8,128)(2,1)}), bf16[64,32,128]{2,1,0:T(8,128)(2,1)S(1)}, u32[]{:S(2)}, u32[]{:S(2)}) async-start(bf16[64,32,128]{2,1,0:T(8,128)(2,1)} %bitcast), calls=%async_computation | async-start | bytes 1048576 | tf_op jit(solution)/shard_map/all_to_all | solution.py:247
  13.5 26.2 %collective-permute-start = (bf16[128,4,128]{2,1,0:T(4,128)(2,1)S(1)}, bf16[128,4,128]{2,1,0:T(4,128)(2,1)S(1)}, u32[]{:S(2)}, u32[]{:S(2)}) collective-permute-start(bf16[128,4,128]{2,1,0:T(4,128)(2,1)S(1)} %copy-done.5), channel_id=1, source_target_pairs={{0,1},{1,0},{2,3},{3,2},{4,5},{5,4},{6,7},{7,6},{8,9},{9,8},{10,11... | collective-permute-start | bytes 393224 | tf_op jit(solution)/shard_map/ppermute | solution.py:244
  14.6 25.2 %collective-permute-start.1 = (bf16[128,4,128]{2,1,0:T(4,128)(2,1)S(1)}, bf16[128,4,128]{2,1,0:T(4,128)(2,1)S(1)}, u32[]{:S(2)}, u32[]{:S(2)}) collective-permute-start(bf16[128,4,128]{2,1,0:T(4,128)(2,1)S(1)} %copy-done.6), channel_id=1, source_target_pairs={{0,1},{1,0},{2,3},{3,2},{4,5},{5,4},{6,7},{7,6},{8,9},{9,8},{10,11... | collective-permute-start | bytes 393224 | tf_op jit(solution)/shard_map/ppermute | solution.py:244
  14.7 11.1 %collective-permute-start.2 = (s32[4]{0:T(128)S(1)}, s32[4]{0:T(128)S(1)}, u32[]{:S(2)}, u32[]{:S(2)}) collective-permute-start(s32[4]{0:T(128)S(1)} %copy-done.3), channel_id=1, source_target_pairs={{0,1},{1,0},{2,3},{3,2},{4,5},{5,4},{6,7},{7,6},{8,9},{9,8},{10,11... | collective-permute-start | bytes 56 | tf_op jit(solution)/shard_map/ppermute | solution.py:244
  25.9 2.9 %collective-permute-start.3 = (bf16[4,32,128]{2,1,0:T(8,128)(2,1)S(1)}, bf16[4,32,128]{2,1,0:T(8,128)(2,1)S(1)}, u32[]{:S(2)}, u32[]{:S(2)}) collective-permute-start(bf16[4,32,128]{2,1,0:T(8,128)(2,1)S(1)} %pick.1), channel_id=1, source_target_pairs={{0,1},{1,0},{2,3},{3,2},{4,5},{5,4},{6,7},{7,6},{8,9},{9,8},{10,11... | collective-permute-start | bytes 98312 | tf_op jit(solution)/shard_map/ppermute | solution.py:244
  28.8 3.4 %copy-start = (bf16[4,2048,4,128]{3,2,1,0:T(4,128)(2,1)S(1)}, bf16[4,2048,4,128]{3,2,1,0:T(4,128)(2,1)}, u32[]{:S(2)}) copy-start(bf16[4,2048,4,128]{3,2,1,0:T(4,128)(2,1)} %param.10) | copy-start | bytes 25165828
  32.2 3.4 %copy-start.1 = (bf16[4,2048,4,128]{3,2,1,0:T(4,128)(2,1)S(1)}, bf16[4,2048,4,128]{3,2,1,0:T(4,128)(2,1)}, u32[]{:S(2)}) copy-start(bf16[4,2048,4,128]{3,2,1,0:T(4,128)(2,1)} %param.11) | copy-start | bytes 25165828
  39.3 1.5 %collective-permute-start.4 = (f32[4,40,128]{2,1,0:T(8,128)S(1)}, f32[4,40,128]{2,1,0:T(8,128)S(1)}, u32[]{:S(2)}, u32[]{:S(2)}) collective-permute-start(f32[4,40,128]{2,1,0:T(8,128)S(1)} %suffix.1.mine_ref), channel_id=1, source_target_pairs={{0,1},{1,0},{2,3},{3,2},{4,5},{5,4},{6,7},{7,6},{8,9},{9,8},{10,11... | collective-permute-start | bytes 245768 | tf_op jit(solution)/shard_map/ppermute | solution.py:244
